TPU v7x, 32 devices: a whole 2x2x4 slice. The times are simulated.
32 devices in a mesh: gx: 4 (over z), gy: 4 (over y, x), gz: 2 (over core).
Axes of the slice: x: 2, y: 2, z: 4, core: 2. Of those that a mesh axis runs over, the one named last changes fastest.
Arguments:
- positions: float32 [3, 64, 64, 512], P(None, 'gx', 'gy', 'gz'), may hold values from -6 to 6
- pair_node: int32 [4, 4, 2, 32, 256], P('gx', 'gy', 'gz'), may hold values from 0 to 255
- pair_line: int32 [4, 4, 2, 32], P('gx', 'gy', 'gz'), may hold values from 0 to 255
- pair_far: int32 [4, 4, 2, 32, 256], P('gx', 'gy', 'gz'), may hold values from 0 to 261, as said below
- far_line: int32 [4, 4, 2, 32], P('gx', 'gy', 'gz'), may hold values from 0 to 483, as said below
- pair_geom: float32 [4, 4, 2, 32, 4, 256], P('gx', 'gy', 'gz'), may hold values from -4 to 4
- live_blocks: int32 [4, 4, 2], P('gx', 'gy', 'gz'), may hold values from 8 to 32, as said below
Outputs:
- corrected: float32 [3, 64, 64, 512], P(None, 'gx', 'gy', 'gz')
- sweep_history: float32 [2, 5], replicated
Inputs may be any that keep to these rules, and one draw needn't show every extreme that they name: `pair_far`: together with far_line: at most one of the three coordinates of node b lies outside the owner block's own nodes; node b lies inside the whole grid; in slots below 16 node b is one of the owner block's own nodes. `far_line`: together with pair_far, as stated there. `live_blocks`: some owner block has all 32 slots live.
All inputs are finite; a program needn't handle non-finite values.
Results may differ from a plain program's by a relative error of at most 0.0001.
Values sent between devices are 32-bit elements; how exact they have to be, the bound alone decides.
A program may use at most 64 MiB of HBM per device.

v0:
```python
import math

import jax
import jax.numpy as jnp
from jax import lax
from jax.sharding import PartitionSpec as P

RIM = 3
SWEEPS = 5


relax_factor = 0.9
highest = lax.Precision.HIGHEST


def extended(cells, sides, width):
    for axis, dim in sides:
        count = lax.axis_size(axis)
        ends = count - 1
        head = lax.slice_in_dim(cells, 0, width, axis=dim)
        tail = lax.slice_in_dim(cells, cells.shape[dim] - width, cells.shape[dim], axis=dim)
        cells = jnp.concatenate(
            [
                lax.ppermute(tail, axis, [(i, (i + 1) % count) for i in range(ends)]),
                cells,
                lax.ppermute(head, axis, [((i + 1) % count, i) for i in range(ends)]),
            ],
            axis=dim,
        )
    return cells


def node_sums(contribs, within, line_index, line_length, count_lines):
    blocks = contribs.shape[0]
    group_size = math.gcd(16, blocks)
    row_count = contribs.shape[1]
    columns = lax.broadcasted_iota(jnp.int32, (1, 1, line_length), 2)
    line_ids = lax.broadcasted_iota(jnp.int32, (1, count_lines), 1)

    def node_add_group(turn_idx, running):
        first_block = turn_idx * group_size
        term_part = lax.dynamic_slice_in_dim(contribs, first_block, group_size, 0)
        node_part = lax.dynamic_slice_in_dim(within, first_block, group_size, 0)
        line_part = lax.dynamic_slice_in_dim(line_index, first_block, group_size, 0)
        one_hot = (node_part[:, :, None] == columns).astype(jnp.float32)
        window = jnp.einsum("bcp,bpn->bcn", term_part, one_hot, precision=highest)
        line_hot = (line_part[:, None] == line_ids).astype(jnp.float32)
        return running + jnp.einsum("bl,bcn->cln", line_hot, window, precision=highest)

    initial = jnp.zeros((row_count, count_lines, line_length), jnp.float32)
    return lax.fori_loop(0, blocks // group_size, node_add_group, initial)


def select_lines(line_hot, field_lines):
    return jnp.einsum("bl,cln->bcn", line_hot, field_lines, precision=highest)


def sweep_terms(
    near_lines, far_lines, within, far_pos, line_index, geometry, live_mask, count_lines
):
    blocks = within.shape[0]
    group_size = math.gcd(16, blocks)
    near_cols = lax.broadcasted_iota(jnp.int32, (1, 1, near_lines.shape[2]), 2)
    far_cols = lax.broadcasted_iota(jnp.int32, (1, 1, far_lines.shape[2]), 2)
    line_ids = lax.broadcasted_iota(jnp.int32, (1, count_lines), 1)

    def sweep_add_group(turn_idx, carry):
        running, energy_sum = carry
        near_hot = (within[:, :, None] == near_cols).astype(jnp.float32)
        far_hot = (far_pos[:, :, None] == far_cols).astype(jnp.float32)
        near_vals = jnp.einsum("bcn,bpn->bcp", near_lines, near_hot, precision=highest)
        far_vals = jnp.einsum("bcn,bpn->bcp", far_lines, far_hot, precision=highest)
        differ = near_vals - far_vals
        gap_value = (
            geometry[:, 0, :] * differ[:, 0, :]
            + geometry[:, 1, :] * differ[:, 1, :]
            + geometry[:, 2, :] * differ[:, 2, :]
            - geometry[:, 3, :]
        )
        depth_value = jnp.where(live_mask, jnp.maximum(-gap_value, 0.0), 0.0)
        contribs = depth_value[:, None, :] * geometry[:, 0:3, :]
        window = jnp.einsum("bcp,bpn->bcn", contribs, near_hot, precision=highest)
        line_hot = (line_index[:, None] == line_ids).astype(jnp.float32)
        running = running + jnp.einsum("bl,bcn->cln", line_hot, window, precision=highest)
        return (running, energy_sum + jnp.sum(depth_value * depth_value))

    initial = (
        jnp.zeros((3, count_lines, near_lines.shape[2]), jnp.float32),
        jnp.zeros((), jnp.float32),
    )
    return lax.fori_loop(0, blocks // group_size, sweep_add_group, initial)


def local(positions, pair_node, pair_line, pair_far, far_line, pair_geom, live_blocks):
    within = pair_node[0, 0, 0]
    line_index = pair_line[0, 0, 0]
    far_pos = pair_far[0, 0, 0]
    far_index = far_line[0, 0, 0]
    geometry = pair_geom[0, 0, 0]
    live_count = live_blocks[0, 0, 0]
    size_x = positions.shape[1]
    size_y = positions.shape[2]
    size_z = positions.shape[3]
    blocks = within.shape[0]
    pair_count = within.shape[1]
    inner_count = blocks // 2
    count_lines = size_x * size_y
    ext_lines = (size_x + 2 * RIM) * (size_y + 2 * RIM)
    ext_z = size_z + 2 * RIM
    devices = lax.axis_size("gx") * lax.axis_size("gy") * lax.axis_size("gz")
    slot_count = blocks * pair_count
    live_mask = lax.broadcasted_iota(jnp.int32, (blocks, 1), 0) < live_count
    near_hot = (line_index[:, None] == lax.broadcasted_iota(jnp.int32, (1, count_lines), 1)).astype(
        jnp.float32
    )
    far_hot = (far_index[:, None] == lax.broadcasted_iota(jnp.int32, (1, ext_lines), 1)).astype(
        jnp.float32
    )
    live_ones = jnp.broadcast_to(
        jnp.where(live_mask, 1.0, 0.0).astype(jnp.float32), (blocks, pair_count)
    )
    counts = node_sums(live_ones[:, None, :], within, line_index, size_z, count_lines).reshape(
        size_x, size_y, size_z
    )
    widths = ((0, 0), (RIM, RIM), (RIM, RIM), (RIM, RIM))
    padded = extended(positions, (("gx", 1), ("gy", 2), ("gz", 3)), RIM)
    current = positions
    energies = []
    residuals = []
    for sweep_idx in range(SWEEPS):
        near_lines = select_lines(near_hot, current.reshape(3, count_lines, size_z))
        local_pad = jnp.pad(current, widths).reshape(3, ext_lines, ext_z)
        inner_far = select_lines(far_hot[:inner_count], local_pad)
        inner_total, inner_energy = sweep_terms(
            near_lines[:inner_count],
            inner_far,
            within[:inner_count],
            far_pos[:inner_count],
            line_index[:inner_count],
            geometry[:inner_count],
            live_mask[:inner_count],
            count_lines,
        )
        outer_far = select_lines(far_hot[inner_count:], padded.reshape(3, ext_lines, ext_z))
        outer_total, outer_energy = sweep_terms(
            near_lines[inner_count:],
            outer_far,
            within[inner_count:],
            far_pos[inner_count:],
            line_index[inner_count:],
            geometry[inner_count:],
            live_mask[inner_count:],
            count_lines,
        )
        node_total = inner_total + outer_total
        energy_local = inner_energy + outer_energy
        total_energy = lax.psum(energy_local, ("gx", "gy", "gz"))
        scale_factor = 1.0 / (1.0 + total_energy / (slot_count * devices))
        correction = (
            relax_factor
            * scale_factor
            * node_total.reshape(3, size_x, size_y, size_z)
            / (1.0 + counts)
        )
        current = current + correction
        residual_local = jnp.sum(correction * correction)
        residuals.append(lax.psum(residual_local, ("gx", "gy", "gz")))
        energies.append(total_energy)
        if sweep_idx + 1 < SWEEPS:
            padded = extended(current, (("gx", 1), ("gy", 2), ("gz", 3)), RIM)
    history = jnp.stack(
        [
            jnp.sqrt(1.0 + jnp.stack(energies) / slot_count),
            jnp.sqrt(1.0 + jnp.stack(residuals) / (size_x * size_y * size_z)),
        ]
    )
    return (current, history)


def solution(mesh):
    return jax.shard_map(
        local,
        mesh=mesh,
        in_specs=(
            P(None, "gx", "gy", "gz"),
            P("gx", "gy", "gz", None, None),
            P("gx", "gy", "gz", None),
            P("gx", "gy", "gz", None, None),
            P("gx", "gy", "gz", None),
            P("gx", "gy", "gz", None, None, None),
            P("gx", "gy", "gz"),
        ),
        out_specs=(P(None, "gx", "gy", "gz"), P()),
        check_vma=False,
    )
```

profile of v0, /device:TPU:0, one launch (start us, length us, event | category | flops | bytes accessed | tf_op | source)
XLA Modules:
  0.0 585.4 jit_solution(6506297491511349636)
XLA Ops:
  3.7 5.6 collective-permute-start
  13.4 3.0 reshape.413
  26.3 4.3 while.9
  33.4 4.6 collective-permute-start.2
  38.0 2.8 fusion.32
  46.5 4.1 collective-permute-start.4
  59.5 2.6 fusion.249
  66.3 44.0 %psum.70 = f32[]{:T(128)} all-reduce(f32[]{:T(128)S(6)} %add.349), channel_id=1, replica_groups=mesh['gx'=4,'gy'=4,'gz'=2] {'gx','gy','gz'}, use_global_device_ids=true, to_apply=%region_2.3 | all-reduce | flops 1 | bytes 8 | tf_op jit(solution)/shard_map/psum | solution.py:157
  114.8 4.6 collective-permute-start.6
  123.5 4.8 collective-permute-start.8
  138.4 3.8 collective-permute-start.10
  142.2 3.6 fusion.30
  147.7 5.1 pad_maximum_fusion.1
  152.8 3.0 reshape.416
  162.3 3.0 reshape.417
  171.9 43.0 %psum.71 = f32[]{:T(128)} all-reduce(f32[]{:T(128)S(6)} %add.359), channel_id=1, replica_groups=mesh['gx'=4,'gy'=4,'gz'=2] {'gx','gy','gz'}, use_global_device_ids=true, to_apply=%region_7.8 | all-reduce | flops 1 | bytes 8 | tf_op jit(solution)/shard_map/psum | solution.py:157
  219.3 5.0 collective-permute-start.12
  228.0 4.8 collective-permute-start.14
  232.9 2.8 fusion.38
  242.1 3.0 collective-permute-start.16
  245.2 3.6 fusion.28
  251.6 5.0 pad_maximum_fusion.2
  256.5 3.0 reshape.419
  259.5 2.5 fusion.242
  269.0 2.5 fusion.247
  276.5 44.2 %psum.72 = f32[]{:T(128)} all-reduce(f32[]{:T(128)S(6)} %add.367), channel_id=1, replica_groups=mesh['gx'=4,'gy'=4,'gz'=2] {'gx','gy','gz'}, use_global_device_ids=true, to_apply=%region_10.11 | all-reduce | flops 1 | bytes 8 | tf_op jit(solution)/shard_map/psum | solution.py:157
  325.2 4.7 collective-permute-start.18
  333.9 4.8 collective-permute-start.20
  348.6 3.7 collective-permute-start.22
  352.3 3.6 fusion.26
  357.8 5.1 pad_maximum_fusion.3
  362.9 3.0 reshape.422
  372.4 3.0 reshape.423
  382.0 43.2 %psum.73 = f32[]{:T(128)} all-reduce(f32[]{:T(128)S(6)} %add.375), channel_id=1, replica_groups=mesh['gx'=4,'gy'=4,'gz'=2] {'gx','gy','gz'}, use_global_device_ids=true, to_apply=%region_13.14 | all-reduce | flops 1 | bytes 8 | tf_op jit(solution)/shard_map/psum | solution.py:157
  429.6 4.8 collective-permute-start.24
  438.3 4.8 collective-permute-start.26
  443.2 2.8 fusion.34
  452.4 3.0 collective-permute-start.28
  455.4 3.6 fusion.24
  461.8 5.0 pad_maximum_fusion.4
  466.8 3.0 reshape.425
  469.8 2.5 fusion.240
  480.0 2.6 fusion.245
  490.1 44.1 %psum.74 = f32[]{:T(128)} all-reduce(f32[]{:T(128)S(6)} %add.383), channel_id=1, replica_groups=mesh['gx'=4,'gy'=4,'gz'=2] {'gx','gy','gz'}, use_global_device_ids=true, to_apply=%region_16.17 | all-reduce | flops 1 | bytes 8 | tf_op jit(solution)/shard_map/psum | solution.py:157
  534.9 3.1 fusion.88
  539.1 39.2 %all-reduce.5 = (f32[1,1]{1,0:T(1,128)}, f32[1,1]{1,0:T(1,128)}, f32[1,1]{1,0:T(1,128)}, f32[1,1]{1,0:T(1,128)}, f32[1,1]{1,0:T(1,128)}) all-reduce(f32[1,1]{1,0:T(1,128)} %bitcast.57, f32[1,1]{1,0:T(1,128)} %bitcast.58, f32[1,1]{1,0:T(1,128)} %bitcast.59, ...), channel_id=1, replica_groups=mesh['gx'=4,'gy'=4,'gz'=2] {'gx','gy','gz'}, use_global_device_ids=true, to_apply=%region_18.19 | all-reduce | flops 5 | bytes 40 | tf_op jit(solution)/shard_map/psum | solution.py:167
  578.3 3.1 stack.52
  581.4 3.1 stack.46
  (378 shorter events, 163.4 us)
Async XLA Ops:
  2.4 29.6 %collective-permute-start.1 = (f32[3,3,16,256]{3,1,2,0:T(4,128)S(1)}, f32[3,3,16,256]{3,1,2,0:T(4,128)S(1)}, u32[]{:S(2)}, u32[]{:S(2)}) collective-permute-start(f32[3,3,16,256]{3,1,2,0:T(4,128)S(1)} %get-tuple-element.616), channel_id=1, source_target_pairs={{8,0},{16,8},{24,16},{9,1},{17,9},{25,17},{10,2},{18,10},{26,18},{... | collective-permute-start | bytes 442376 | tf_op jit(solution)/shard_map/ppermute | solution.py:26
  3.7 28.3 %collective-permute-start = (f32[3,3,16,256]{3,1,2,0:T(4,128)S(1)}, f32[3,3,16,256]{3,1,2,0:T(4,128)S(1)}, u32[]{:S(2)}, u32[]{:S(2)}) collective-permute-start(f32[3,3,16,256]{3,1,2,0:T(4,128)S(1)} %get-tuple-element.615), channel_id=1, source_target_pairs={{0,8},{8,16},{16,24},{1,9},{9,17},{17,25},{2,10},{10,18},{18,26},{... | collective-permute-start | bytes 442376 | tf_op jit(solution)/shard_map/ppermute | solution.py:24
  10.1 14.4 %copy-start.55 = (s32[16,256]{1,0:T(8,128)}, s32[16,256]{1,0:T(8,128)S(1)}, u32[]{:S(2)}) copy-start(s32[16,256]{1,0:T(8,128)S(1)} %get-tuple-element.637) | copy-start | bytes 49156
  10.1 27.9 %copy-start.52 = (s32[16,256]{1,0:T(8,128)}, s32[16,256]{1,0:T(8,128)S(1)}, u32[]{:S(2)}) copy-start(s32[16,256]{1,0:T(8,128)S(1)} %get-tuple-element.636) | copy-start | bytes 49156
  16.6 42.9 %copy-start.30 = (pred[32,484]{1,0:T(8,128)(4,1)}, pred[32,484]{1,0:T(8,128)(4,1)S(1)}, u32[]{:S(2)}) copy-start(pred[32,484]{1,0:T(8,128)(4,1)S(1)} %iota_compare_fusion.40) | copy-start | bytes 46468
  17.1 13.4 %copy-start.48 = (s32[16]{0:T(128)}, s32[16]{0:T(128)S(1)}, u32[]{:S(2)}) copy-start(s32[16]{0:T(128)S(1)} %get-tuple-element.643) | copy-start | bytes 196
  32.1 9.3 %collective-permute-start.3 = (f32[3,22,3,256]{3,1,2,0:T(8,128)S(1)}, f32[3,22,3,256]{3,1,2,0:T(8,128)S(1)}, u32[]{:S(2)}, u32[]{:S(2)}) collective-permute-start(f32[3,22,3,256]{3,1,2,0:T(8,128)S(1)} %get-tuple-element.590), channel_id=1, source_target_pairs={{2,0},{4,2},{6,4},{3,1},{5,3},{7,5},{10,8},{12,10},{14,12},{11,9},... | collective-permute-start | bytes 608264 | tf_op jit(solution)/shard_map/ppermute | solution.py:26
  33.4 8.7 %collective-permute-start.2 = (f32[3,22,3,256]{3,1,2,0:T(8,128)S(1)}, f32[3,22,3,256]{3,1,2,0:T(8,128)S(1)}, u32[]{:S(2)}, u32[]{:S(2)}) collective-permute-start(f32[3,22,3,256]{3,1,2,0:T(8,128)S(1)} %get-tuple-element.589), channel_id=1, source_target_pairs={{0,2},{2,4},{4,6},{1,3},{3,5},{5,7},{8,10},{10,12},{12,14},{9,11},... | collective-permute-start | bytes 608264 | tf_op jit(solution)/shard_map/ppermute | solution.py:24
  44.5 8.3 %collective-permute-start.5 = (f32[3,22,22,3]{2,1,3,0:T(8,128)}, f32[3,22,22,3]{2,1,3,0:T(8,128)S(1)}, u32[]{:S(2)}, u32[]{:S(2)}) collective-permute-start(f32[3,22,22,3]{2,1,3,0:T(8,128)} %copy.270), channel_id=1, source_target_pairs={{1,0},{3,2},{5,4},{7,6},{9,8},{11,10},{13,12},{15,14},{17,16},{19,... | collective-permute-start | bytes 52280 | tf_op jit(solution)/shard_map/ppermute | solution.py:26
  46.5 7.0 %collective-permute-start.4 = (f32[3,22,22,3]{2,1,3,0:T(8,128)S(1)}, f32[3,22,22,3]{2,1,3,0:T(8,128)}, u32[]{:S(2)}, u32[]{:S(2)}) collective-permute-start(f32[3,22,22,3]{2,1,3,0:T(8,128)S(1)} %copy.269), channel_id=1, source_target_pairs={{0,1},{2,3},{4,5},{6,7},{8,9},{10,11},{12,13},{14,15},{16,17},{18,... | collective-permute-start | bytes 52280 | tf_op jit(solution)/shard_map/ppermute | solution.py:24
  59.4 51.5 %copy-start.53 = (s32[16,256]{1,0:T(8,128)S(1)}, s32[16,256]{1,0:T(8,128)}, u32[]{:S(2)}) copy-start(s32[16,256]{1,0:T(8,128)} %copy-done.52) | copy-start | bytes 49156
  59.4 53.2 %copy-start.13 = (f32[3,256,256]{1,2,0:T(8,128)S(1)}, f32[3,256,256]{1,2,0:T(8,128)}, u32[]{:S(2)}) copy-start(f32[3,256,256]{1,2,0:T(8,128)} %fusion.132) | copy-start | bytes 2359300
  59.4 53.2 %copy-start.70 = (s32[16]{0:T(128)S(1)}, s32[16]{0:T(128)}, u32[]{:S(2)}) copy-start(s32[16]{0:T(128)} %get-tuple-element.642) | copy-start | bytes 196
  113.4 14.9 %copy-start.56 = (s32[16,256]{1,0:T(8,128)S(1)}, s32[16,256]{1,0:T(8,128)}, u32[]{:S(2)}) copy-start(s32[16,256]{1,0:T(8,128)} %copy-done.55) | copy-start | bytes 49156
  113.5 7.0 %collective-permute-start.7 = (f32[3,3,16,256]{3,2,1,0:T(8,128)S(1)}, f32[3,3,16,256]{3,2,1,0:T(8,128)S(1)}, u32[]{:S(2)}, u32[]{:S(2)}) collective-permute-start(f32[3,3,16,256]{3,2,1,0:T(8,128)S(1)} %get-tuple-element.614), channel_id=1, source_target_pairs={{8,0},{16,8},{24,16},{9,1},{17,9},{25,17},{10,2},{18,10},{26,18},{... | collective-permute-start | bytes 442376 | tf_op jit(solution)/shard_map/ppermute | solution.py:26
  114.8 7.2 %collective-permute-start.6 = (f32[3,3,16,256]{3,2,1,0:T(8,128)S(1)}, f32[3,3,16,256]{3,2,1,0:T(8,128)S(1)}, u32[]{:S(2)}, u32[]{:S(2)}) collective-permute-start(f32[3,3,16,256]{3,2,1,0:T(8,128)S(1)} %get-tuple-element.613), channel_id=1, source_target_pairs={{0,8},{8,16},{16,24},{1,9},{9,17},{17,25},{2,10},{10,18},{18,26},{... | collective-permute-start | bytes 442376 | tf_op jit(solution)/shard_map/ppermute | solution.py:24
  122.1 9.7 %collective-permute-start.9 = (f32[3,22,3,256]{3,1,2,0:T(8,128)S(1)}, f32[3,22,3,256]{3,1,2,0:T(8,128)S(1)}, u32[]{:S(2)}, u32[]{:S(2)}) collective-permute-start(f32[3,22,3,256]{3,1,2,0:T(8,128)S(1)} %copy.294), channel_id=1, source_target_pairs={{2,0},{4,2},{6,4},{3,1},{5,3},{7,5},{10,8},{12,10},{14,12},{11,9},... | collective-permute-start | bytes 608264 | tf_op jit(solution)/shard_map/ppermute | solution.py:26
  123.5 8.4 %collective-permute-start.8 = (f32[3,22,3,256]{3,1,2,0:T(8,128)S(1)}, f32[3,22,3,256]{3,1,2,0:T(8,128)S(1)}, u32[]{:S(2)}, u32[]{:S(2)}) collective-permute-start(f32[3,22,3,256]{3,1,2,0:T(8,128)S(1)} %copy.293), channel_id=1, source_target_pairs={{0,2},{2,4},{4,6},{1,3},{3,5},{5,7},{8,10},{10,12},{12,14},{9,11},... | collective-permute-start | bytes 608264 | tf_op jit(solution)/shard_map/ppermute | solution.py:24
  135.4 10.4 %collective-permute-start.11 = (f32[3,22,22,3]{2,1,3,0:T(8,128)S(1)}, f32[3,22,22,3]{2,1,3,0:T(8,128)S(1)}, u32[]{:S(2)}, u32[]{:S(2)}) collective-permute-start(f32[3,22,22,3]{2,1,3,0:T(8,128)S(1)} %copy.298), channel_id=1, source_target_pairs={{1,0},{3,2},{5,4},{7,6},{9,8},{11,10},{13,12},{15,14},{17,16},{19,... | collective-permute-start | bytes 52280 | tf_op jit(solution)/shard_map/ppermute | solution.py:26
  138.4 7.9 %collective-permute-start.10 = (f32[3,22,22,3]{2,1,3,0:T(8,128)S(1)}, f32[3,22,22,3]{2,1,3,0:T(8,128)}, u32[]{:S(2)}, u32[]{:S(2)}) collective-permute-start(f32[3,22,22,3]{2,1,3,0:T(8,128)S(1)} %copy.297), channel_id=1, source_target_pairs={{0,1},{2,3},{4,5},{6,7},{8,9},{10,11},{12,13},{14,15},{16,17},{18,... | collective-permute-start | bytes 52280 | tf_op jit(solution)/shard_map/ppermute | solution.py:24
  165.3 51.8 %copy-start.71 = (s32[16]{0:T(128)S(1)}, s32[16]{0:T(128)}, u32[]{:S(2)}) copy-start(s32[16]{0:T(128)} %get-tuple-element.642) | copy-start | bytes 196
  218.0 14.9 %copy-start.58 = (s32[16,256]{1,0:T(8,128)S(1)}, s32[16,256]{1,0:T(8,128)}, u32[]{:S(2)}) copy-start(s32[16,256]{1,0:T(8,128)} %copy-done.55) | copy-start | bytes 49156
  218.0 7.3 %collective-permute-start.13 = (f32[3,3,16,256]{3,2,1,0:T(8,128)S(1)}, f32[3,3,16,256]{3,2,1,0:T(8,128)S(1)}, u32[]{:S(2)}, u32[]{:S(2)}) collective-permute-start(f32[3,3,16,256]{3,2,1,0:T(8,128)S(1)} %get-tuple-element.610), channel_id=1, source_target_pairs={{8,0},{16,8},{24,16},{9,1},{17,9},{25,17},{10,2},{18,10},{26,18},{... | collective-permute-start | bytes 442376 | tf_op jit(solution)/shard_map/ppermute | solution.py:26
  219.3 7.2 %collective-permute-start.12 = (f32[3,3,16,256]{3,2,1,0:T(8,128)S(1)}, f32[3,3,16,256]{3,2,1,0:T(8,128)S(1)}, u32[]{:S(2)}, u32[]{:S(2)}) collective-permute-start(f32[3,3,16,256]{3,2,1,0:T(8,128)S(1)} %get-tuple-element.609), channel_id=1, source_target_pairs={{0,8},{8,16},{16,24},{1,9},{9,17},{17,25},{2,10},{10,18},{18,26},{... | collective-permute-start | bytes 442376 | tf_op jit(solution)/shard_map/ppermute | solution.py:24
  226.7 9.0 %collective-permute-start.15 = (f32[3,22,3,256]{3,1,2,0:T(8,128)S(1)}, f32[3,22,3,256]{3,1,2,0:T(8,128)S(1)}, u32[]{:S(2)}, u32[]{:S(2)}) collective-permute-start(f32[3,22,3,256]{3,1,2,0:T(8,128)S(1)} %copy.320), channel_id=1, source_target_pairs={{2,0},{4,2},{6,4},{3,1},{5,3},{7,5},{10,8},{12,10},{14,12},{11,9},... | collective-permute-start | bytes 608264 | tf_op jit(solution)/shard_map/ppermute | solution.py:26
  228.0 8.3 %collective-permute-start.14 = (f32[3,22,3,256]{3,1,2,0:T(8,128)S(1)}, f32[3,22,3,256]{3,1,2,0:T(8,128)S(1)}, u32[]{:S(2)}, u32[]{:S(2)}) collective-permute-start(f32[3,22,3,256]{3,1,2,0:T(8,128)S(1)} %copy.319), channel_id=1, source_target_pairs={{0,2},{2,4},{4,6},{1,3},{3,5},{5,7},{8,10},{10,12},{12,14},{9,11},... | collective-permute-start | bytes 608264 | tf_op jit(solution)/shard_map/ppermute | solution.py:24
  240.3 8.5 %collective-permute-start.17 = (f32[3,22,22,3]{2,1,3,0:T(8,128)S(1)}, f32[3,22,22,3]{2,1,3,0:T(8,128)S(1)}, u32[]{:S(2)}, u32[]{:S(2)}) collective-permute-start(f32[3,22,22,3]{2,1,3,0:T(8,128)S(1)} %copy.324), channel_id=1, source_target_pairs={{1,0},{3,2},{5,4},{7,6},{9,8},{11,10},{13,12},{15,14},{17,16},{19,... | collective-permute-start | bytes 52280 | tf_op jit(solution)/shard_map/ppermute | solution.py:26
  242.1 8.0 %collective-permute-start.16 = (f32[3,22,22,3]{2,1,3,0:T(8,128)S(1)}, f32[3,22,22,3]{2,1,3,0:T(8,128)S(1)}, u32[]{:S(2)}, u32[]{:S(2)}) collective-permute-start(f32[3,22,22,3]{2,1,3,0:T(8,128)S(1)} %copy.323), channel_id=1, source_target_pairs={{0,1},{2,3},{4,5},{6,7},{8,9},{10,11},{12,13},{14,15},{16,17},{18,... | collective-permute-start | bytes 52280 | tf_op jit(solution)/shard_map/ppermute | solution.py:24
  269.0 52.4 %copy-start.54 = (s32[16,256]{1,0:T(8,128)S(1)}, s32[16,256]{1,0:T(8,128)}, u32[]{:S(2)}) copy-start(s32[16,256]{1,0:T(8,128)} %copy-done.52) | copy-start | bytes 49156
  269.0 54.0 %copy-start.72 = (s32[16]{0:T(128)S(1)}, s32[16]{0:T(128)}, u32[]{:S(2)}) copy-start(s32[16]{0:T(128)} %get-tuple-element.642) | copy-start | bytes 196
  323.8 14.9 %copy-start.60 = (s32[16,256]{1,0:T(8,128)S(1)}, s32[16,256]{1,0:T(8,128)}, u32[]{:S(2)}) copy-start(s32[16,256]{1,0:T(8,128)} %copy-done.55) | copy-start | bytes 49156
  323.9 7.1 %collective-permute-start.19 = (f32[3,3,16,256]{3,2,1,0:T(8,128)S(1)}, f32[3,3,16,256]{3,2,1,0:T(8,128)S(1)}, u32[]{:S(2)}, u32[]{:S(2)}) collective-permute-start(f32[3,3,16,256]{3,2,1,0:T(8,128)S(1)} %get-tuple-element.606), channel_id=1, source_target_pairs={{8,0},{16,8},{24,16},{9,1},{17,9},{25,17},{10,2},{18,10},{26,18},{... | collective-permute-start | bytes 442376 | tf_op jit(solution)/shard_map/ppermute | solution.py:26
  325.2 7.2 %collective-permute-start.18 = (f32[3,3,16,256]{3,2,1,0:T(8,128)S(1)}, f32[3,3,16,256]{3,2,1,0:T(8,128)S(1)}, u32[]{:S(2)}, u32[]{:S(2)}) collective-permute-start(f32[3,3,16,256]{3,2,1,0:T(8,128)S(1)} %get-tuple-element.605), channel_id=1, source_target_pairs={{0,8},{8,16},{16,24},{1,9},{9,17},{17,25},{2,10},{10,18},{18,26},{... | collective-permute-start | bytes 442376 | tf_op jit(solution)/shard_map/ppermute | solution.py:24
  332.5 9.5 %collective-permute-start.21 = (f32[3,22,3,256]{3,1,2,0:T(8,128)S(1)}, f32[3,22,3,256]{3,1,2,0:T(8,128)S(1)}, u32[]{:S(2)}, u32[]{:S(2)}) collective-permute-start(f32[3,22,3,256]{3,1,2,0:T(8,128)S(1)} %copy.346), channel_id=1, source_target_pairs={{2,0},{4,2},{6,4},{3,1},{5,3},{7,5},{10,8},{12,10},{14,12},{11,9},... | collective-permute-start | bytes 608264 | tf_op jit(solution)/shard_map/ppermute | solution.py:26
  333.9 8.3 %collective-permute-start.20 = (f32[3,22,3,256]{3,1,2,0:T(8,128)S(1)}, f32[3,22,3,256]{3,1,2,0:T(8,128)S(1)}, u32[]{:S(2)}, u32[]{:S(2)}) collective-permute-start(f32[3,22,3,256]{3,1,2,0:T(8,128)S(1)} %copy.345), channel_id=1, source_target_pairs={{0,2},{2,4},{4,6},{1,3},{3,5},{5,7},{8,10},{10,12},{12,14},{9,11},... | collective-permute-start | bytes 608264 | tf_op jit(solution)/shard_map/ppermute | solution.py:24
  345.7 10.2 %collective-permute-start.23 = (f32[3,22,22,3]{2,1,3,0:T(8,128)S(1)}, f32[3,22,22,3]{2,1,3,0:T(8,128)S(1)}, u32[]{:S(2)}, u32[]{:S(2)}) collective-permute-start(f32[3,22,22,3]{2,1,3,0:T(8,128)S(1)} %copy.350), channel_id=1, source_target_pairs={{1,0},{3,2},{5,4},{7,6},{9,8},{11,10},{13,12},{15,14},{17,16},{19,... | collective-permute-start | bytes 52280 | tf_op jit(solution)/shard_map/ppermute | solution.py:26
  348.6 7.8 %collective-permute-start.22 = (f32[3,22,22,3]{2,1,3,0:T(8,128)S(1)}, f32[3,22,22,3]{2,1,3,0:T(8,128)}, u32[]{:S(2)}, u32[]{:S(2)}) collective-permute-start(f32[3,22,22,3]{2,1,3,0:T(8,128)S(1)} %copy.349), channel_id=1, source_target_pairs={{0,1},{2,3},{4,5},{6,7},{8,9},{10,11},{12,13},{14,15},{16,17},{18,... | collective-permute-start | bytes 52280 | tf_op jit(solution)/shard_map/ppermute | solution.py:24
  375.5 52.0 %copy-start.73 = (s32[16]{0:T(128)S(1)}, s32[16]{0:T(128)}, u32[]{:S(2)}) copy-start(s32[16]{0:T(128)} %get-tuple-element.642) | copy-start | bytes 196
  428.3 14.9 %copy-start.62 = (s32[16,256]{1,0:T(8,128)S(1)}, s32[16,256]{1,0:T(8,128)}, u32[]{:S(2)}) copy-start(s32[16,256]{1,0:T(8,128)} %copy-done.55) | copy-start | bytes 49156
  428.3 7.1 %collective-permute-start.25 = (f32[3,3,16,256]{3,2,1,0:T(8,128)S(1)}, f32[3,3,16,256]{3,2,1,0:T(8,128)S(1)}, u32[]{:S(2)}, u32[]{:S(2)}) collective-permute-start(f32[3,3,16,256]{3,2,1,0:T(8,128)S(1)} %get-tuple-element.602), channel_id=1, source_target_pairs={{8,0},{16,8},{24,16},{9,1},{17,9},{25,17},{10,2},{18,10},{26,18},{... | collective-permute-start | bytes 442376 | tf_op jit(solution)/shard_map/ppermute | solution.py:26
  429.6 7.2 %collective-permute-start.24 = (f32[3,3,16,256]{3,2,1,0:T(8,128)S(1)}, f32[3,3,16,256]{3,2,1,0:T(8,128)S(1)}, u32[]{:S(2)}, u32[]{:S(2)}) collective-permute-start(f32[3,3,16,256]{3,2,1,0:T(8,128)S(1)} %get-tuple-element.601), channel_id=1, source_target_pairs={{0,8},{8,16},{16,24},{1,9},{9,17},{17,25},{2,10},{10,18},{18,26},{... | collective-permute-start | bytes 442376 | tf_op jit(solution)/shard_map/ppermute | solution.py:24
  437.0 9.0 %collective-permute-start.27 = (f32[3,22,3,256]{3,1,2,0:T(8,128)S(1)}, f32[3,22,3,256]{3,1,2,0:T(8,128)S(1)}, u32[]{:S(2)}, u32[]{:S(2)}) collective-permute-start(f32[3,22,3,256]{3,1,2,0:T(8,128)S(1)} %copy.372), channel_id=1, source_target_pairs={{2,0},{4,2},{6,4},{3,1},{5,3},{7,5},{10,8},{12,10},{14,12},{11,9},... | collective-permute-start | bytes 608264 | tf_op jit(solution)/shard_map/ppermute | solution.py:26
  438.3 8.3 %collective-permute-start.26 = (f32[3,22,3,256]{3,1,2,0:T(8,128)S(1)}, f32[3,22,3,256]{3,1,2,0:T(8,128)S(1)}, u32[]{:S(2)}, u32[]{:S(2)}) collective-permute-start(f32[3,22,3,256]{3,1,2,0:T(8,128)S(1)} %copy.371), channel_id=1, source_target_pairs={{0,2},{2,4},{4,6},{1,3},{3,5},{5,7},{8,10},{10,12},{12,14},{9,11},... | collective-permute-start | bytes 608264 | tf_op jit(solution)/shard_map/ppermute | solution.py:24
  450.6 8.5 %collective-permute-start.29 = (f32[3,22,22,3]{2,1,3,0:T(8,128)S(1)}, f32[3,22,22,3]{2,1,3,0:T(8,128)S(1)}, u32[]{:S(2)}, u32[]{:S(2)}) collective-permute-start(f32[3,22,22,3]{2,1,3,0:T(8,128)S(1)} %copy.376), channel_id=1, source_target_pairs={{1,0},{3,2},{5,4},{7,6},{9,8},{11,10},{13,12},{15,14},{17,16},{19,... | collective-permute-start | bytes 52280 | tf_op jit(solution)/shard_map/ppermute | solution.py:26
  452.4 8.0 %collective-permute-start.28 = (f32[3,22,22,3]{2,1,3,0:T(8,128)S(1)}, f32[3,22,22,3]{2,1,3,0:T(8,128)S(1)}, u32[]{:S(2)}, u32[]{:S(2)}) collective-permute-start(f32[3,22,22,3]{2,1,3,0:T(8,128)S(1)} %copy.375), channel_id=1, source_target_pairs={{0,1},{2,3},{4,5},{6,7},{8,9},{10,11},{12,13},{14,15},{16,17},{18,... | collective-permute-start | bytes 52280 | tf_op jit(solution)/shard_map/ppermute | solution.py:24
  480.0 54.8 %copy-start.7 = (f32[3,256,256]{1,2,0:T(8,128)S(1)}, f32[3,256,256]{1,2,0:T(8,128)}, u32[]{:S(2)}) copy-start(f32[3,256,256]{1,2,0:T(8,128)} %copy-done.6) | copy-start | bytes 2359300
  480.0 54.8 %copy-start.9 = (f32[3,256,256]{1,2,0:T(8,128)S(1)}, f32[3,256,256]{1,2,0:T(8,128)}, u32[]{:S(2)}) copy-start(f32[3,256,256]{1,2,0:T(8,128)} %copy-done.8) | copy-start | bytes 2359300
  480.0 54.8 %copy-start.11 = (f32[3,256,256]{1,2,0:T(8,128)S(1)}, f32[3,256,256]{1,2,0:T(8,128)}, u32[]{:S(2)}) copy-start(f32[3,256,256]{1,2,0:T(8,128)} %copy-done.10) | copy-start | bytes 2359300
  (57 other events, 343.4 us)
where the time goes:
time: 595 us; the launch traced here: 585 us
  blocking collectives  258 us (43%)
  matrix products  107 us (18%)
  starting transfers between devices  85.6 us (14%)
  local copies, waits for them, and re-layouts  75.5 us (13%)
  other arithmetic  37.2 us (6%)
  between operations  12.3 us (2%)
  waiting for transfers between devices  10.5 us (2%)
    psum x5, blocking collectives, local(): total_energy = lax.psum(energy_local, ('gx', 'gy', 'gz'))  218 us
    ppermute x15, starting transfers between devices, extended(): lax.ppermute(tail, axis, [(i, (i + 1) % count) for i in range(ends)])  66.1 us
    psum x1, blocking collectives, local(): residuals.append(lax.psum(residual_local, ('gx', 'gy', 'gz')))  39.2 us
    dot_general x10, matrix products, sweep_add_group(): jnp.einsum('bcn,bpn->bcp', near_lines, near_hot, precision=highest)  29.1 us
    dot_general x15, matrix products, select_lines(): return jnp.einsum('bl,cln->bcn', line_hot, field_lines, precision=highest)  27.3 us
    concatenate x10, other arithmetic, extended(): jnp.concatenate([lax.ppermute(tail, axis, [(i, (i + 1) % count) for i in...  23.8 us
    ppermute x15, starting transfers between devices, extended(): lax.ppermute(head, axis, [((i + 1) % count, i) for i in range(ends)])  19.5 us
    dot_general x10, matrix products, sweep_add_group(): far_vals = jnp.einsum('bcn,bpn->bcp', far_lines, far_hot, precision=highest)  18.4 us
  transfers between devices with their start and end apart: 30, of which 11 were waited for; matrix products, arithmetic and copies ran while one was open for 11% of the time, Pallas kernels for 0%

commit v1 on v0

v1 whole, which is shorter than its diff:
```python
import functools

import jax
import jax.numpy as jnp
from jax import lax
from jax.experimental import pallas as pl
from jax.experimental.pallas import tpu as pltpu
from jax.sharding import PartitionSpec as P

RIM = 3
SWEEPS = 5
RELAX = 0.9
AXES = ("gx", "gy", "gz")
MESH = pl.DeviceIdType.MESH
f32 = jnp.float32
bf16 = jnp.bfloat16


def split(x, parts):
    out = []
    for _ in range(parts - 1):
        hi = x.astype(bf16)
        out.append(hi)
        x = x - hi.astype(f32)
    out.append(x.astype(bf16))
    return out


def mm(a, b):
    return jnp.dot(a, b, preferred_element_type=f32)


def take_lanes(x, low, half):
    outs = []
    for h in range(0, low.shape[1], 128):
        idx = low[:, h : h + 128]
        got = jnp.take_along_axis(x[:, :128], idx, axis=1, mode="promise_in_bounds")
        for j in range(1, x.shape[1] // 128):
            more = jnp.take_along_axis(
                x[:, 128 * j : 128 * (j + 1)], idx, axis=1, mode="promise_in_bounds"
            )
            got = jnp.where(half[:, h : h + 128] == j, more, got)
        outs.append(got)
    return jnp.concatenate(outs, axis=1)


def kernel(
    sizes,
    blk,
    live_ref,
    pk_ref,
    pos_ref,
    out_ref,
    hist_ref,
    hot,
    two,
    amat,
    cinv,
    geo,
    low_ref,
    half_ref,
    gap,
    acc,
    wcat,
    reqs,
    dsend,
    drecv,
    erecv,
    rrecv,
    evals,
    qs_sem,
    qr_sem,
    ds_sem,
    dr_sem,
    es_sem,
    er_sem,
    rs_sem,
    rr_sem,
):
    nx, ny, nz = sizes
    bx, by, bz = blk
    devices = nx * ny * nz
    blocks = pk_ref.shape[1]
    pairs = pk_ref.shape[2]
    outer = blocks // 2
    lines = bx * by
    me = [lax.axis_index(a) for a in AXES]
    mine = (me[0] * ny + me[1]) * nz + me[2]
    dirs = [(a, s) for a in range(3) for s in (1, -1)]

    def neighbour(axis, sign):
        to = list(me)
        to[axis] = lax.rem(me[axis] + sign + sizes[axis], sizes[axis])
        return tuple(to)

    def coords(k):
        to = lax.rem(mine + k, devices)
        return (to // (ny * nz), lax.rem(to // nz, ny), lax.rem(to, nz))

    for d, (axis, sign) in enumerate(dirs):
        pltpu.make_async_remote_copy(
            src_ref=pk_ref.at[pl.ds(0, 5), pl.ds(outer, outer)],
            dst_ref=reqs.at[d],
            send_sem=qs_sem,
            recv_sem=qr_sem,
            device_id=neighbour(axis, sign),
            device_id_type=MESH,
        ).start()

    live = live_ref[0]
    live_rows = lax.broadcasted_iota(jnp.int32, (blocks, pairs), 0) < live
    lane_node = lax.broadcasted_iota(jnp.int32, (pairs, bz), 1).astype(f32)
    node_t = jnp.transpose(pk_ref[6])
    for b in range(blocks):
        hot[pl.ds(b * pairs, pairs), :] = jnp.where(
            node_t[:, b : b + 1] == lane_node, 1.0, 0.0
        ).astype(bf16)
    line_b = pk_ref[7]
    two[...] = jnp.transpose(jnp.concatenate([line_b, line_b], axis=0))
    row_mod = lax.broadcasted_iota(jnp.int32, (blocks, 2 * blocks), 0)
    col_mod = lax.rem(lax.broadcasted_iota(jnp.int32, (blocks, 2 * blocks), 1), blocks)
    same = line_b[:, : 2 * blocks] == two[0:blocks, :]
    first_row = 1.0 - jnp.max(
        jnp.where(same & (row_mod < col_mod), 1.0, 0.0), axis=0, keepdims=True
    )
    first_col = 1.0 - jnp.max(
        jnp.where(same & (col_mod < row_mod), 1.0, 0.0), axis=1, keepdims=True
    )
    line_rows = lax.broadcasted_iota(jnp.int32, (lines, 2 * blocks), 0).astype(f32)
    lane_line = lax.broadcasted_iota(jnp.int32, (blocks, lines), 1).astype(f32)

    def expand(stack, step):
        rows = stack.shape[0]
        which = lax.rem(lax.broadcasted_iota(jnp.int32, (rows, pairs), 0), step)
        return jnp.concatenate(
            [jnp.where(which == j, stack, 0.0).astype(bf16) for j in range(step)], axis=1
        )

    counts = []
    for g in range(blocks // 8):
        ones = jnp.where(live_rows[8 * g : 8 * g + 8], 1.0, 0.0)
        counts.append(mm(expand(ones, 8), hot[pl.ds(8 * g * pairs, 8 * pairs), :]))
    counts = jnp.concatenate(counts, axis=0).astype(bf16)

    pos_parts = [split(pos_ref[c].reshape(lines, bz), 3) for c in range(3)]

    def setup(row, n, line, node, valid, geom, sign):
        sel = line[:, : 2 * blocks] == two[0:n, :]
        a = jnp.where(sel, 1.0, 0.0)
        amat[pl.ds(row, n), :] = a.astype(bf16)
        cnt = mm(a[:, :blocks].astype(bf16), counts)
        cinv[pl.ds(row, n), :] = RELAX / (1.0 + cnt)
        idx = jnp.where(valid, node, 0.0).astype(jnp.int32)
        low_ref[pl.ds(row, n), :] = lax.rem(idx, 128)
        half_ref[pl.ds(row, n), :] = idx // 128
        own = jnp.where(line == lane_line[:n], 1.0, 0.0).astype(bf16)
        total = jnp.zeros((n, pairs), f32)
        for c in range(3):
            gc = jnp.where(valid, geom[c], 0.0) * sign
            geo[c, pl.ds(row, n), :] = gc
            vals = mm(own, pos_parts[c][0]) + mm(own, pos_parts[c][1]) + mm(own, pos_parts[c][2])
            total += gc * take_lanes(vals, low_ref[pl.ds(row, n), :], half_ref[pl.ds(row, n), :])
        return total

    def located(code, zpos, shift):
        e = jnp.floor((code + 0.5) / (by + 2 * RIM))
        f = code - e * (by + 2 * RIM)
        e = e - (RIM + shift[0] * bx)
        f = f - (RIM + shift[1] * by)
        z = zpos - (RIM + shift[2] * bz)
        ok_line = (e >= 0) & (e < bx) & (f >= 0) & (f < by)
        return jnp.where(ok_line, e * by + f, -1.0), z, ok_line & (z >= 0) & (z < bz)

    geom_own = [pk_ref[c] for c in range(3)]
    start = setup(0, blocks, line_b, pk_ref[6], line_b >= 0, geom_own, 1.0)
    line, z, ok = located(pk_ref[4], pk_ref[3], (0, 0, 0))
    start += setup(blocks, blocks, line, z, ok, geom_own, -1.0)
    gap[...] = start - pk_ref[5]
    acc[...] = jnp.zeros_like(acc)

    pltpu.make_async_copy(reqs, reqs, qr_sem).wait()
    base = 2 * blocks
    for d, (axis, sign) in enumerate(dirs):
        shift = [0, 0, 0]
        shift[axis] = sign
        line, z, ok = located(reqs[d, 4], reqs[d, 3], shift)
        geom = [reqs[d, c] for c in range(3)]
        dsend[0, d] = setup(base + d * outer, outer, line, z, ok, geom, -1.0)

    def respond(t):
        for d, (axis, sign) in enumerate(dirs):
            pltpu.make_async_remote_copy(
                src_ref=dsend.at[t, d],
                dst_ref=drecv.at[t, d],
                send_sem=ds_sem.at[t],
                recv_sem=dr_sem.at[t],
                device_id=neighbour(axis, -sign),
                device_id_type=MESH,
            ).start()

    def received(t):
        pltpu.make_async_copy(drecv.at[t], drecv.at[t], dr_sem.at[t]).wait()
        got = drecv[t, 0]
        for d in range(1, len(dirs)):
            got = got + drecv[t, d]
        return got

    respond(0)
    gap[pl.ds(outer, outer), :] = gap[pl.ds(outer, outer), :] + received(0)

    def to_all(ref, send_sem, recv_sem):
        def send(k, carry):
            pltpu.make_async_remote_copy(
                src_ref=ref,
                dst_ref=ref,
                send_sem=send_sem,
                recv_sem=recv_sem,
                device_id=coords(k),
                device_id_type=MESH,
            ).start()
            return carry

        lax.fori_loop(1, devices, send, 0)

    def lanes_sum(x):
        x = jnp.sum(x, axis=0, keepdims=True)
        out = x[:, :128]
        for j in range(1, x.shape[1] // 128):
            out = out + x[:, 128 * j : 128 * (j + 1)]
        return out

    def sweep(t, last):
        depth = jnp.where(live_rows, jnp.maximum(-gap[...], 0.0), 0.0)
        erecv[t, mine] = lanes_sum(depth * depth)
        to_all(erecv.at[t, mine], es_sem.at[t], er_sem.at[t])
        for g in range(blocks // 8):
            lo, hi = 8 * g, 8 * g + 8
            terms = jnp.concatenate([depth[lo:hi] * pk_ref[c, lo:hi] for c in range(3)], axis=0)
            top = terms.astype(bf16).astype(f32)
            stack = jnp.concatenate([top, terms - top], axis=0)
            sums = mm(expand(stack, 8), hot[pl.ds(lo * pairs, 8 * pairs), :])
            sums = sums[:24] + sums[24:]
            for c in range(3):
                wcat[lo:hi, c * bz : (c + 1) * bz] = sums[8 * c : 8 * c + 8]
        parts = jnp.concatenate(split(wcat[...], 2), axis=0)
        rows = blocks if last else amat.shape[0]
        both = mm(amat[0:rows, :], parts)
        moved = [both[:, c * bz : (c + 1) * bz] * cinv[0:rows, :] for c in range(3)]
        near = jnp.concatenate([m[:blocks] for m in moved], axis=1)
        rrecv[mine, pl.ds(t, 1), :] = lanes_sum(near * near * first_col)
        if last:
            to_all(rrecv.at[mine], rs_sem, rr_sem)
        else:
            total = geo[0] * take_lanes(moved[0], low_ref[...], half_ref[...])
            for c in range(1, 3):
                total += geo[c] * take_lanes(moved[c], low_ref[...], half_ref[...])
            for d in range(len(dirs)):
                dsend[t + 1, d] = total[base + d * outer : base + (d + 1) * outer]
            respond(t + 1)
            step = total[:blocks] + total[blocks : 2 * blocks]
        others = erecv.at[t, pl.ds(0, devices - 1)]
        pltpu.make_async_copy(others, others, er_sem.at[t]).wait()
        energy = jnp.sum(jnp.sum(erecv[t], axis=0), axis=1, keepdims=True)
        scale = 1.0 / (1.0 + energy / (blocks * pairs * devices))
        evals[0, pl.ds(t, 1), :] = jnp.broadcast_to(energy, (1, 128))
        evals[1, pl.ds(t, 1), :] = jnp.broadcast_to(scale, (1, 128))
        acc[...] = acc[...] + scale * near
        if not last:
            more = received(t + 1)
            gap[0:outer, :] = gap[0:outer, :] + scale * step[:outer]
            gap[pl.ds(outer, outer), :] = gap[pl.ds(outer, outer), :] + scale * (
                step[outer:] + more
            )

    rrecv[mine] = jnp.zeros(rrecv.shape[1:], f32)
    evals[...] = jnp.zeros_like(evals)

    def body(t, carry):
        sweep(t, False)
        return carry

    lax.fori_loop(0, SWEEPS - 1, body, 0)
    sweep(SWEEPS - 1, True)

    place = jnp.where(line_rows == two[...], 1.0, 0.0) * first_row
    place = place.astype(bf16)
    total = mm(place, jnp.concatenate(split(acc[...], 2), axis=0))
    for c in range(3):
        out_ref[c] = pos_ref[c] + total[:, c * bz : (c + 1) * bz].reshape(bx, by, bz)

    others = rrecv.at[pl.ds(0, devices - 1)]
    pltpu.make_async_copy(others, others, rr_sem).wait()
    resid = jnp.sum(jnp.sum(rrecv[...], axis=0), axis=1, keepdims=True)
    scales = evals[1]
    hist_ref[0] = jnp.sqrt(1.0 + evals[0] / (blocks * pairs))
    hist_ref[1] = jnp.sqrt(1.0 + scales * scales * resid / (bx * by * bz))

    pltpu.make_async_copy(reqs, reqs, qs_sem).wait()
    for t in range(SWEEPS):
        pltpu.make_async_copy(dsend.at[t], dsend.at[t], ds_sem.at[t]).wait()
        ref = erecv.at[t, pl.ds(0, devices - 1)]
        pltpu.make_async_copy(ref, ref, es_sem.at[t]).wait()
    pltpu.make_async_copy(others, others, rs_sem).wait()


def local(sizes, positions, pair_node, pair_line, pair_far, far_line, pair_geom, live_blocks):
    within = pair_node[0, 0, 0]
    blocks, pairs = within.shape
    blk = positions.shape[1:]
    geometry = jnp.moveaxis(pair_geom[0, 0, 0], 1, 0)

    def wide(x):
        return jnp.broadcast_to(x[:, None], (blocks, pairs)).astype(f32)

    packed = jnp.stack(
        [
            geometry[0],
            geometry[1],
            geometry[2],
            pair_far[0, 0, 0].astype(f32),
            wide(far_line[0, 0, 0]),
            geometry[3],
            within.astype(f32),
            wide(pair_line[0, 0, 0]),
        ]
    )
    devices = sizes[0] * sizes[1] * sizes[2]
    outer = blocks // 2
    rows = 2 * blocks + 6 * outer
    dma = pltpu.SemaphoreType.DMA
    vmem = pl.BlockSpec(memory_space=pltpu.VMEM)
    corrected, hist = pl.pallas_call(
        functools.partial(kernel, sizes, blk),
        out_shape=(
            jax.ShapeDtypeStruct(positions.shape, f32),
            jax.ShapeDtypeStruct((2, 8, 128), f32),
        ),
        in_specs=[pl.BlockSpec(memory_space=pltpu.SMEM), vmem, vmem],
        out_specs=(vmem, vmem),
        scratch_shapes=[
            pltpu.VMEM((blocks * pairs, blk[2]), bf16),
            pltpu.VMEM((pairs, 2 * blocks), f32),
            pltpu.VMEM((rows, 2 * blocks), bf16),
            pltpu.VMEM((rows, pairs), f32),
            pltpu.VMEM((3, rows, pairs), f32),
            pltpu.VMEM((rows, pairs), jnp.int32),
            pltpu.VMEM((rows, pairs), jnp.int32),
            pltpu.VMEM((blocks, pairs), f32),
            pltpu.VMEM((blocks, 3 * blk[2]), f32),
            pltpu.VMEM((blocks, 3 * blk[2]), f32),
            pltpu.VMEM((6, 5, outer, pairs), f32),
            pltpu.VMEM((SWEEPS, 6, outer, pairs), f32),
            pltpu.VMEM((SWEEPS, 6, outer, pairs), f32),
            pltpu.VMEM((SWEEPS, devices, 1, 128), f32),
            pltpu.VMEM((devices, 8, 128), f32),
            pltpu.VMEM((2, 8, 128), f32),
            dma,
            dma,
            dma((SWEEPS,)),
            dma((SWEEPS,)),
            dma((SWEEPS,)),
            dma((SWEEPS,)),
            dma,
            dma,
        ],
        compiler_params=pltpu.CompilerParams(has_side_effects=True),
    )(live_blocks.reshape(1), packed, positions)
    return corrected, hist[:, :SWEEPS, 0]


def solution(mesh):
    sizes = tuple(mesh.shape[a] for a in AXES)
    return jax.shard_map(
        functools.partial(local, sizes),
        mesh=mesh,
        in_specs=(
            P(None, "gx", "gy", "gz"),
            P("gx", "gy", "gz", None, None),
            P("gx", "gy", "gz", None),
            P("gx", "gy", "gz", None, None),
            P("gx", "gy", "gz", None),
            P("gx", "gy", "gz", None, None, None),
            P("gx", "gy", "gz"),
        ),
        out_specs=(P(None, "gx", "gy", "gz"), P()),
        check_vma=False,
    )
```

time: 595 us -> 62.7 us (0.11); the launches traced: 585 us -> 62.3 us
  blocking collectives: 258 us -> 0 us
  matrix products: 107 us -> 0 us
  starting transfers between devices: 85.6 us -> 0 us
  local copies, waits for them, and re-layouts: 75.5 us -> 7.99 us
  Pallas kernels: 0 us -> 53 us
  other arithmetic: 37.2 us -> 0.01 us
  between operations: 12.3 us -> 1.32 us
  waiting for transfers between devices: 10.5 us -> 0 us
    psum x6 -> x0, blocking collectives: 258 us -> none  [the longest x5 218 us: local(): total_energy = lax.psum(energy_local, ('gx', 'gy', 'gz'))]
    dot_general x59 -> x0, matrix products: 107 us -> none  [the longest x10 29.1 us: sweep_add_group(): jnp.einsum('bcn,bpn->bcp', near_lines, near_hot, precision=highest)]
    ppermute x30 -> x0, starting transfers between devices: 85.6 us -> none  [the longest x15 66.1 us: extended(): lax.ppermute(tail, axis, [(i, (i + 1) % count) for i in range(ends)])]
    pallas_call x0 -> x1, Pallas kernels: none -> 53 us  [local(): pl.pallas_call(functools.partial(kernel, sizes, blk), out_shape=(jax.Shap...]
    reshape x10 -> x0, local copies, waits for them, and re-layouts: 25.9 us -> none  [the longest x5 15 us: local(): local_pad = jnp.pad(current, widths).reshape(3, ext_lines, ext_z)]
    concatenate x10 -> x0, other arithmetic: 23.8 us -> none  [extended(): jnp.concatenate([lax.ppermute(tail, axis, [(i, (i + 1) % count) for i in...]
    slice x36 -> x1, local copies, waits for them, and re-layouts: 21.2 us -> 1.35 us  [local(): return (corrected, hist[:, :SWEEPS, 0])]
    ppermute x18 -> x0, local copies, waits for them, and re-layouts: 12.4 us -> none  [the longest x9 7.57 us: extended(): lax.ppermute(tail, axis, [(i, (i + 1) % count) for i in range(ends)])]
  transfers between devices with their start and end apart: 30 -> 0, of which waited for: 11 -> 0; matrix products, arithmetic and copies ran while one was open for 11% -> 0% of each run, Pallas kernels for 0% -> 0%
where the time goes in v1:
time: 62.7 us; the launch traced here: 62.3 us
  Pallas kernels  53 us (85%)
  local copies, waits for them, and re-layouts  7.99 us (13%)
  between operations  1.32 us (2%)
    pallas_call x1, Pallas kernels, local(): pl.pallas_call(functools.partial(kernel, sizes, blk), out_shape=(jax.Shap...  53 us
    unnamed x15, local copies, waits for them, and re-layouts  6.57 us
    slice x1, local copies, waits for them, and re-layouts, local(): return (corrected, hist[:, :SWEEPS, 0])  1.35 us

profile of v1, /device:TPU:0, one launch (start us, length us, event | category | flops | bytes accessed | tf_op | source)
XLA Modules:
  0.0 62.3 jit_solution(14705008266415154733)
XLA Ops:
  1.3 0.0 copy-start.3
  1.3 0.6 %copy-done.3 = s32[1,1,1,32]{3,2,1,0:T(1,128)S(1)} copy-done((s32[1,1,1,32]{3,2,1,0:T(1,128)S(1)}, s32[1,1,1,32]{3,2,1,0:T(1,128)}, u32[]{:S(2)}) %copy-start.3) | copy-done | bytes 152
  1.9 0.0 copy-start.4
  1.9 0.7 %copy-done.4 = s32[1,1,1,32]{3,2,1,0:T(1,128)S(1)} copy-done((s32[1,1,1,32]{3,2,1,0:T(1,128)S(1)}, s32[1,1,1,32]{3,2,1,0:T(1,128)}, u32[]{:S(2)}) %copy-start.4) | copy-done | bytes 152
  2.6 0.9 %copy.12 = f32[1,1,1,32,4,256]{5,3,4,2,1,0:T(8,128)S(1)} copy(f32[1,1,1,32,4,256]{5,4,3,2,1,0:T(4,128)} %param.12) | data formatting | bytes 262144 | tf_op args[5]
  3.5 0.0 copy-start.1
  3.6 0.7 %copy-done.1 = s32[1,1,1,32,256]{4,3,2,1,0:T(8,128)S(1)} copy-done((s32[1,1,1,32,256]{4,3,2,1,0:T(8,128)S(1)}, s32[1,1,1,32,256]{4,3,2,1,0:T(8,128)}, u32[]{:S(2)}) %copy-start.1) | copy-done | bytes 32792
  4.3 0.1 broadcast_dynamic-update-slice_fusion.1
  4.4 0.0 copy-start.2
  4.4 0.8 %copy-done.2 = s32[1,1,1,32,256]{4,3,2,1,0:T(8,128)S(1)} copy-done((s32[1,1,1,32,256]{4,3,2,1,0:T(8,128)S(1)}, s32[1,1,1,32,256]{4,3,2,1,0:T(8,128)}, u32[]{:S(2)}) %copy-start.2) | copy-done | bytes 32792
  5.1 0.1 broadcast_dynamic-update-slice_fusion.pk_ref
  5.2 0.0 copy-start
  5.2 0.7 %copy-done = f32[8,32,256]{2,1,0:T(8,128)} copy-done((f32[8,32,256]{2,1,0:T(8,128)}, f32[8,32,256]{2,1,0:T(8,128)S(1)}, u32[]{:S(2)}) %copy-start) | copy-done | bytes 262168
  5.9 53.0 %shard_map.86 = (f32[3,16,16,256]{3,2,1,0:T(8,128)}, f32[2,8,128]{2,1,0:T(8,128)}) custom-call(s32[1]{0:T(128)} %bitcast.14.live_ref, f32[8,32,256]{2,1,0:T(8,128)} %copy-done, f32[3,16,16,256]{3,2,1,0:T(8,128)} %pos_ref.1), custom_call_target="tpu_custom_call" | custom-call | tf_op jit(solution)/shard_map/pallas_call | solution.py:332
  58.9 1.3 %slice_reduce_fusion = f32[2,5]{1,0:T(2,128)} fusion(f32[2,8,128]{2,1,0:T(8,128)} %get-tuple-element.5), kind=kLoop, calls=%fused_computation.7 | loop fusion | bytes 80 | tf_op jit(solution)/shard_map/slice | solution.py:368
  60.2 2.1 %copy.20 = f32[3,16,16,256]{3,2,1,0:T(8,128)} copy(f32[3,16,16,256]{3,2,1,0:T(8,128)} %get-tuple-element.8) | data formatting | bytes 1572864
  (6 shorter events, 0.0 us)
Async XLA Ops:
  1.3 0.7 %copy-start.3 = (s32[1,1,1,32]{3,2,1,0:T(1,128)S(1)}, s32[1,1,1,32]{3,2,1,0:T(1,128)}, u32[]{:S(2)}) copy-start(s32[1,1,1,32]{3,2,1,0:T(1,128)} %param.9) | copy-start | bytes 388
  1.9 0.7 %copy-start.4 = (s32[1,1,1,32]{3,2,1,0:T(1,128)S(1)}, s32[1,1,1,32]{3,2,1,0:T(1,128)}, u32[]{:S(2)}) copy-start(s32[1,1,1,32]{3,2,1,0:T(1,128)} %param.11) | copy-start | bytes 388
  3.5 0.8 %copy-start.1 = (s32[1,1,1,32,256]{4,3,2,1,0:T(8,128)S(1)}, s32[1,1,1,32,256]{4,3,2,1,0:T(8,128)}, u32[]{:S(2)}) copy-start(s32[1,1,1,32,256]{4,3,2,1,0:T(8,128)} %param.10) | copy-start | bytes 98308
  4.4 0.8 %copy-start.2 = (s32[1,1,1,32,256]{4,3,2,1,0:T(8,128)S(1)}, s32[1,1,1,32,256]{4,3,2,1,0:T(8,128)}, u32[]{:S(2)}) copy-start(s32[1,1,1,32,256]{4,3,2,1,0:T(8,128)} %param.8) | copy-start | bytes 98308
  5.2 0.7 %copy-start = (f32[8,32,256]{2,1,0:T(8,128)}, f32[8,32,256]{2,1,0:T(8,128)S(1)}, u32[]{:S(2)}) copy-start(f32[8,32,256]{2,1,0:T(8,128)S(1)} %broadcast_dynamic-update-slice_fusion.pk_ref) | copy-start | bytes 786436

commit v2 on v1

v2 whole, which is shorter than its diff:
```python
import functools

import jax
import jax.numpy as jnp
from jax import lax
from jax.experimental import pallas as pl
from jax.experimental.pallas import tpu as pltpu
from jax.sharding import PartitionSpec as P

RIM = 3
SWEEPS = 5
RELAX = 0.9
AXES = ("gx", "gy", "gz")
MESH = pl.DeviceIdType.MESH
f32 = jnp.float32
bf16 = jnp.bfloat16


def split(x, parts):
    out = []
    for _ in range(parts - 1):
        hi = x.astype(bf16)
        out.append(hi)
        x = x - hi.astype(f32)
    out.append(x.astype(bf16))
    return out


def mm(a, b):
    return jnp.dot(a, b, preferred_element_type=f32)


def take_lanes(x, low, half):
    outs = []
    for h in range(0, low.shape[1], 128):
        idx = low[:, h : h + 128]
        got = jnp.take_along_axis(x[:, :128], idx, axis=1, mode="promise_in_bounds")
        for j in range(1, x.shape[1] // 128):
            more = jnp.take_along_axis(
                x[:, 128 * j : 128 * (j + 1)], idx, axis=1, mode="promise_in_bounds"
            )
            got = jnp.where(half[:, h : h + 128] == j, more, got)
        outs.append(got)
    return jnp.concatenate(outs, axis=1)


def kernel(
    sizes,
    blk,
    live_ref,
    node_ref,
    line_ref,
    farpos_ref,
    farline_ref,
    geom_ref,
    pos_hbm,
    acc_ref,
    hist_ref,
    pos_ref,
    req,
    cols,
    hot,
    two,
    amat,
    cinv,
    geo,
    low_ref,
    half_ref,
    gap,
    wcat,
    reqs,
    dsend,
    drecv,
    erecv,
    rrecv,
    pos_sem,
    qs_sem,
    qr_sem,
    ds_sem,
    dr_sem,
    es_sem,
    er_sem,
    rs_sem,
    rr_sem,
):
    nx, ny, nz = sizes
    bx, by, bz = blk
    devices = nx * ny * nz
    blocks, pairs = gap.shape
    outer = blocks // 2
    lines = bx * by
    me = [lax.axis_index(a) for a in AXES]
    mine = (me[0] * ny + me[1]) * nz + me[2]
    dirs = [(a, s) for a in range(3) for s in (1, -1)]

    def neighbour(axis, sign):
        to = list(me)
        to[axis] = lax.rem(me[axis] + sign + sizes[axis], sizes[axis])
        return tuple(to)

    def coords(k):
        to = lax.rem(mine + k, devices)
        return (to // (ny * nz), lax.rem(to // nz, ny), lax.rem(to, nz))

    pos_copy = pltpu.make_async_copy(pos_hbm, pos_ref, pos_sem)
    pos_copy.start()

    def column(ref):
        row = ref[0, 0].astype(f32)
        return jnp.transpose(jnp.broadcast_to(row, (pairs, blocks)))

    for c in range(3):
        req[c] = geom_ref[0, 0, 0, outer:, c, :]
    req[3] = farpos_ref[0, 0, 0, outer:, :].astype(f32)
    cols[1] = column(farline_ref)
    req[4] = cols[1, outer:, :]
    cols[0] = column(line_ref)
    for d, (axis, sign) in enumerate(dirs):
        pltpu.make_async_remote_copy(
            src_ref=req,
            dst_ref=reqs.at[d],
            send_sem=qs_sem,
            recv_sem=qr_sem,
            device_id=neighbour(axis, sign),
            device_id_type=MESH,
        ).start()

    live = jnp.broadcast_to(live_ref[0], (blocks, pairs))
    live_rows = lax.broadcasted_iota(jnp.int32, (blocks, pairs), 0) < live
    lane_node = lax.broadcasted_iota(jnp.int32, (pairs, bz), 1).astype(f32)
    node_t = jnp.transpose(node_ref[0, 0, 0].astype(f32))
    for b in range(blocks):
        hot[pl.ds(b * pairs, pairs), :] = jnp.where(
            node_t[:, b : b + 1] == lane_node, 1.0, 0.0
        ).astype(bf16)
    row_line = line_ref[0, 0].astype(f32)
    two[...] = jnp.concatenate([row_line, row_line], axis=1)
    row_mod = lax.broadcasted_iota(jnp.int32, (blocks, blocks), 0)
    col_mod = lax.broadcasted_iota(jnp.int32, (blocks, blocks), 1)
    line_b = cols[0]
    same = line_b[:, :blocks] == row_line
    first_col = 1.0 - jnp.max(
        jnp.where(same & (col_mod < row_mod), 1.0, 0.0), axis=1, keepdims=True
    )

    def expand(stack, step):
        rows = stack.shape[0]
        which = lax.rem(lax.broadcasted_iota(jnp.int32, (rows, pairs), 0), step)
        return jnp.concatenate(
            [jnp.where(which == j, stack, 0.0).astype(bf16) for j in range(step)], axis=1
        )

    counts = []
    for g in range(blocks // 8):
        ones = jnp.where(live_rows[8 * g : 8 * g + 8], 1.0, 0.0)
        counts.append(mm(expand(ones, 8), hot[pl.ds(8 * g * pairs, 8 * pairs), :]))
    counts = jnp.concatenate(counts, axis=0).astype(bf16)

    def located(code, zpos, shift):
        e = jnp.floor((code + 0.5) / (by + 2 * RIM))
        f = code - e * (by + 2 * RIM)
        e = e - (RIM + shift[0] * bx)
        f = f - (RIM + shift[1] * by)
        z = zpos - (RIM + shift[2] * bz)
        ok_line = (e >= 0) & (e < bx) & (f >= 0) & (f < by)
        return jnp.where(ok_line, e * by + f, -1.0), z, ok_line & (z >= 0) & (z < bz)

    def setup(row, line, node, geom):
        n = line.shape[0]
        lane_line = lax.broadcasted_iota(jnp.int32, (n, lines), 1).astype(f32)
        a = jnp.where(line[:, : 2 * blocks] == two[...], 1.0, 0.0).astype(bf16)
        amat[pl.ds(row, n), :] = a
        cinv[pl.ds(row, n), :] = RELAX / (1.0 + mm(a[:, :blocks], counts))
        idx = node.astype(jnp.int32)
        low = lax.bitwise_and(idx, 127)
        half = lax.shift_right_logical(idx, 7)
        low_ref[pl.ds(row, n), :] = low
        half_ref[pl.ds(row, n), :] = half
        own = jnp.where(line == lane_line, 1.0, 0.0).astype(bf16)
        total = jnp.zeros((n, pairs), f32)
        for c in range(3):
            geo[c, pl.ds(row, n), :] = geom[c]
            vals = jnp.zeros((n, bz), f32)
            for part in split(pos_ref[c].reshape(lines, bz), 3):
                vals += mm(own, part)
            total += geom[c] * take_lanes(vals, low, half)
        return total

    def cat(parts):
        return jnp.concatenate(parts, axis=0)

    pos_copy.wait()
    pltpu.make_async_copy(reqs, reqs, qr_sem).wait()
    asked = []
    for d, (axis, sign) in enumerate(dirs):
        shift = [0, 0, 0]
        shift[axis] = sign
        line, z, ok = located(reqs[d, 4], reqs[d, 3], shift)
        asked.append(
            [line, jnp.where(ok, z, 0.0)] + [jnp.where(ok, -reqs[d, c], 0.0) for c in range(3)]
        )
    asked = [cat([x[i] for x in asked]) for i in range(5)]
    base = asked[0].shape[0]
    rows = base + 2 * blocks

    def respond(t, total):
        for d, (axis, sign) in enumerate(dirs):
            dsend[t, d] = total[d * outer : (d + 1) * outer]
        for d, (axis, sign) in enumerate(dirs):
            pltpu.make_async_remote_copy(
                src_ref=dsend.at[t, d],
                dst_ref=drecv.at[t, d],
                send_sem=ds_sem.at[t],
                recv_sem=dr_sem.at[t],
                device_id=neighbour(axis, -sign),
                device_id_type=MESH,
            ).start()

    def received(t):
        pltpu.make_async_copy(drecv.at[t], drecv.at[t], dr_sem.at[t]).wait()
        got = drecv[t, 0]
        for d in range(1, len(dirs)):
            got = got + drecv[t, d]
        return got

    respond(0, setup(0, asked[0], asked[1], asked[2:]))

    line, z, ok = located(cols[1], farpos_ref[0, 0, 0].astype(f32), (0, 0, 0))
    geom = [geom_ref[0, 0, 0, :, c, :] for c in range(4)]
    start = setup(
        base,
        cat([line_b, line]),
        cat([node_ref[0, 0, 0].astype(f32), jnp.where(ok, z, 0.0)]),
        [cat([geom[c], jnp.where(ok, -geom[c], 0.0)]) for c in range(3)],
    )
    start = start[:blocks] + start[blocks:] - geom[3]
    gap[0:outer, :] = start[:outer]
    gap[pl.ds(outer, outer), :] = start[outer:] + received(0)
    acc_ref[...] = jnp.zeros_like(acc_ref)

    def to_all(ref, send_sem, recv_sem):
        def send(k, carry):
            pltpu.make_async_remote_copy(
                src_ref=ref,
                dst_ref=ref,
                send_sem=send_sem,
                recv_sem=recv_sem,
                device_id=coords(k),
                device_id_type=MESH,
            ).start()
            return carry

        lax.fori_loop(1, devices, send, 0)

    def lanes_sum(x):
        x = jnp.sum(x, axis=0, keepdims=True)
        out = x[:, :128]
        for j in range(1, x.shape[1] // 128):
            out = out + x[:, 128 * j : 128 * (j + 1)]
        return out

    lane = lax.broadcasted_iota(jnp.int32, (1, 128), 1)

    def apply(row, n, parts):
        both = mm(amat[row : row + n, :], parts)
        return [both[:, c * bz : (c + 1) * bz] * cinv[row : row + n, :] for c in range(3)]

    def dots(row, n, moved):
        low = low_ref[row : row + n, :]
        half = half_ref[row : row + n, :]
        total = geo[0, row : row + n] * take_lanes(moved[0], low, half)
        for c in range(1, 3):
            total += geo[c, row : row + n] * take_lanes(moved[c], low, half)
        return total

    def sweep(t, last):
        depth = jnp.where(live_rows, jnp.maximum(-gap[...], 0.0), 0.0)
        erecv[t, mine] = lanes_sum(depth * depth)
        to_all(erecv.at[t, mine], es_sem.at[t], er_sem.at[t])
        for g in range(blocks // 8):
            lo, hi = 8 * g, 8 * g + 8
            terms = cat([depth[lo:hi] * geo[c, base + lo : base + hi] for c in range(3)])
            top = terms.astype(bf16).astype(f32)
            sums = mm(expand(cat([top, terms - top]), 8), hot[pl.ds(lo * pairs, 8 * pairs), :])
            sums = sums[:24] + sums[24:]
            for c in range(3):
                wcat[lo:hi, c * bz : (c + 1) * bz] = sums[8 * c : 8 * c + 8]
        parts = cat(split(wcat[...], 2))
        if not last:
            respond(t + 1, dots(0, base, apply(0, base, parts)))
        moved = apply(base, blocks if last else 2 * blocks, parts)
        near = jnp.concatenate([m[:blocks] for m in moved], axis=1)
        resid = jnp.sum(lanes_sum(near * near * first_col), axis=1, keepdims=True)
        rrecv[mine] = jnp.where(lane == t, resid, rrecv[mine])
        if last:
            to_all(rrecv.at[mine], rs_sem, rr_sem)
        else:
            step = dots(base, 2 * blocks, moved)
            step = step[:blocks] + step[blocks:]
        others = erecv.at[t, pl.ds(0, devices - 1)]
        pltpu.make_async_copy(others, others, er_sem.at[t]).wait()
        energy = jnp.sum(jnp.sum(erecv[t], axis=0), axis=1, keepdims=True)
        scale = 1.0 / (1.0 + energy / (blocks * pairs * devices))
        hist_ref[0:1, :] = jnp.where(lane == t, energy, hist_ref[0:1, :])
        hist_ref[1:2, :] = jnp.where(lane == t, scale, hist_ref[1:2, :])
        acc_ref[...] = acc_ref[...] + (scale * first_col) * near
        if not last:
            more = received(t + 1)
            gap[0:outer, :] = gap[0:outer, :] + scale * step[:outer]
            gap[pl.ds(outer, outer), :] = gap[pl.ds(outer, outer), :] + scale * (
                step[outer:] + more
            )

    rrecv[mine] = jnp.zeros((1, 128), f32)
    hist_ref[...] = jnp.zeros_like(hist_ref)

    def body(t, carry):
        sweep(t, False)
        return carry

    lax.fori_loop(0, SWEEPS - 1, body, 0)
    sweep(SWEEPS - 1, True)

    pltpu.make_async_copy(reqs, reqs, qs_sem).wait()
    for t in range(SWEEPS):
        pltpu.make_async_copy(dsend.at[t], dsend.at[t], ds_sem.at[t]).wait()
        ref = erecv.at[t, pl.ds(0, devices - 1)]
        pltpu.make_async_copy(ref, ref, es_sem.at[t]).wait()
    others = rrecv.at[pl.ds(0, devices - 1)]
    pltpu.make_async_copy(others, others, rs_sem).wait()
    pltpu.make_async_copy(others, others, rr_sem).wait()
    energy, scale = hist_ref[0:1, :], hist_ref[1:2, :]
    resid = jnp.sum(rrecv[...], axis=0)
    hist_ref[0:1, :] = jnp.sqrt(1.0 + energy / (blocks * pairs))
    hist_ref[1:2, :] = jnp.sqrt(1.0 + scale * scale * resid / (bx * by * bz))


def finish(acc_ref, line_ref, hist_in, pos_ref, out_ref, hist_ref):
    _, bx, by, bz = pos_ref.shape
    lines = bx * by
    row = line_ref[0, 0].astype(f32)
    row = jnp.concatenate([row, row], axis=1)
    rows = lax.broadcasted_iota(jnp.int32, (lines, row.shape[1]), 0).astype(f32)
    place = jnp.where(rows == row, 1.0, 0.0).astype(bf16)
    total = mm(place, jnp.concatenate(split(acc_ref[...], 2), axis=0))
    out_ref[0] = pos_ref[0] + total.reshape(bx, by, bz)
    hist_ref[...] = hist_in[0:2, : hist_ref.shape[1]]


def local(sizes, positions, pair_node, pair_line, pair_far, far_line, pair_geom, live_blocks):
    blocks, pairs = pair_node.shape[3:]
    blk = positions.shape[1:]
    devices = sizes[0] * sizes[1] * sizes[2]
    outer = blocks // 2
    rows = 2 * blocks + 6 * outer
    dma = pltpu.SemaphoreType.DMA
    vmem = pl.BlockSpec(memory_space=pltpu.VMEM)
    moved, hist = pl.pallas_call(
        functools.partial(kernel, sizes, blk),
        out_shape=(
            jax.ShapeDtypeStruct((blocks, 3 * blk[2]), f32),
            jax.ShapeDtypeStruct((8, 128), f32),
        ),
        in_specs=[vmem] * 6

        + [pl.BlockSpec(memory_space=pl.ANY)],
        out_specs=(vmem, vmem),
        scratch_shapes=[
            pltpu.VMEM(positions.shape, f32),
            pltpu.VMEM((5, outer, pairs), f32),
            pltpu.VMEM((2, blocks, pairs), f32),
            pltpu.VMEM((blocks * pairs, blk[2]), bf16),
            pltpu.VMEM((1, 2 * blocks), f32),
            pltpu.VMEM((rows, 2 * blocks), bf16),
            pltpu.VMEM((rows, pairs), f32),
            pltpu.VMEM((3, rows, pairs), f32),
            pltpu.VMEM((rows, pairs), jnp.int32),
            pltpu.VMEM((rows, pairs), jnp.int32),
            pltpu.VMEM((blocks, pairs), f32),
            pltpu.VMEM((blocks, 3 * blk[2]), f32),
            pltpu.VMEM((6, 5, outer, pairs), f32),
            pltpu.VMEM((SWEEPS, 6, outer, pairs), f32),
            pltpu.VMEM((SWEEPS, 6, outer, pairs), f32),
            pltpu.VMEM((SWEEPS, devices, 1, 128), f32),
            pltpu.VMEM((devices, 1, 128), f32),
            dma,
            dma,
            dma,
            dma((SWEEPS,)),
            dma((SWEEPS,)),
            dma((SWEEPS,)),
            dma((SWEEPS,)),
            dma,
            dma,
        ],
        compiler_params=pltpu.CompilerParams(has_side_effects=True),
    )(live_blocks, pair_node, pair_line, pair_far, far_line, pair_geom, positions)
    return pl.pallas_call(
        finish,
        grid=(3,),
        out_shape=(
            jax.ShapeDtypeStruct(positions.shape, f32),
            jax.ShapeDtypeStruct((2, SWEEPS), f32),
        ),
        in_specs=[
            pl.BlockSpec((blocks, blk[2]), lambda c: (0, c)),
            pl.BlockSpec(pair_line.shape, lambda c: (0, 0, 0, 0)),
            pl.BlockSpec((8, 128), lambda c: (0, 0)),
            pl.BlockSpec((1,) + blk, lambda c: (c, 0, 0, 0)),
        ],
        out_specs=(
            pl.BlockSpec((1,) + blk, lambda c: (c, 0, 0, 0)),
            pl.BlockSpec((2, SWEEPS), lambda c: (0, 0)),
        ),
    )(moved, pair_line, hist, positions)


def solution(mesh):
    sizes = tuple(mesh.shape[a] for a in AXES)
    return jax.shard_map(
        functools.partial(local, sizes),
        mesh=mesh,
        in_specs=(
            P(None, "gx", "gy", "gz"),
            P("gx", "gy", "gz", None, None),
            P("gx", "gy", "gz", None),
            P("gx", "gy", "gz", None, None),
            P("gx", "gy", "gz", None),
            P("gx", "gy", "gz", None, None, None),
            P("gx", "gy", "gz"),
        ),
        out_specs=(P(None, "gx", "gy", "gz"), P()),
        check_vma=False,
    )
```

time: 62.7 us -> 56.1 us (0.89)
  local copies, waits for them, and re-layouts: 7.99 us -> 0 us
  Pallas kernels: 53 us -> 54.6 us
    unnamed x15 -> x0, local copies, waits for them, and re-layouts: 6.57 us -> none
    pallas_call x0 -> x1, Pallas kernels: none -> 3.24 us  [local(): pl.pallas_call(finish, grid=(3,), out_shape=(jax.ShapeDtypeStruct(positio...]
    pallas_call x1, Pallas kernels: 53 us -> 51.4 us  [local(): pl.pallas_call(functools.partial(kernel, sizes, blk), out_shape=(jax.Shap...]
    slice x1 -> x0, local copies, waits for them, and re-layouts: 1.35 us -> none  [local(): return (corrected, hist[:, :SWEEPS, 0])]
where the time goes in v2:
time: 56.1 us; the launch traced here: 55.9 us
  Pallas kernels  54.6 us (97%)
  between operations  1.29 us (2%)
    pallas_call x1, Pallas kernels, local(): pl.pallas_call(functools.partial(kernel, sizes, blk), out_shape=(jax.Shap...  51.4 us
    pallas_call x1, Pallas kernels, local(): pl.pallas_call(finish, grid=(3,), out_shape=(jax.ShapeDtypeStruct(positio...  3.24 us

profile of v2, /device:TPU:0, one launch (start us, length us, event | category | flops | bytes accessed | tf_op | source)
XLA Modules:
  0.0 55.9 jit_solution(10018977629871262649)
XLA Ops:
  1.3 51.4 %shard_map.86 = (f32[32,768]{1,0:T(8,128)}, f32[8,128]{1,0:T(8,128)}) custom-call(s32[1,1,1]{2,1,0:T(1,128)S(6)} %copy.9.live_ref, s32[1,1,1,32,256]{4,3,2,1,0:T(8,128)} %node_ref.1, s32[1,1,1,32]{3,2,1,0:T(1,128)} %line_ref.3, s32[1,1,1,32,256]{4,3,2,1,0:T(8,128)} %farpos_ref.1, s32[1,1,1,32]{3,2,1,0:T(1,128)} %farline_ref.1, ...), custom_call_target="tpu_custom_call" | custom-call | tf_op jit(solution)/shard_map/pallas_call | solution.py:358
  52.7 3.2 %shard_map.87 = (f32[3,16,16,256]{3,2,1,0:T(8,128)}, f32[2,5]{1,0:T(2,128)}) custom-call(f32[32,768]{1,0:T(8,128)} %get-tuple-element.4.acc_ref, s32[1,1,1,32]{3,2,1,0:T(1,128)} %line_ref.3, f32[8,128]{1,0:T(8,128)} %get-tuple-element.5.hist_in, f32[3,16,16,256]{3,2,1,0:T(8,128)} %pos_ref.1), custom_call_target="tpu_custom_call" | custom-call | tf_op jit(solution)/shard_map/pallas_call | solution.py:398

commit v3 on v2

--- a/solution.py
+++ b/solution.py
@@ -91,12 +91,15 @@
     lines = bx * by
     me = [lax.axis_index(a) for a in AXES]
     mine = (me[0] * ny + me[1]) * nz + me[2]
-    dirs = [(a, s) for a in range(3) for s in (1, -1)]
+    dirs = [(a, s) for a in (1, 0, 2) for s in (1, -1)]
 
     def neighbour(axis, sign):
         to = list(me)
         to[axis] = lax.rem(me[axis] + sign + sizes[axis], sizes[axis])
         return tuple(to)
+
+    def exists(axis, sign):
+        return (me[axis] + sign >= 0) & (me[axis] + sign < sizes[axis])
 
     def coords(k):
         to = lax.rem(mine + k, devices)
@@ -115,15 +118,32 @@
     cols[1] = column(farline_ref)
     req[4] = cols[1, outer:, :]
     cols[0] = column(line_ref)
-    for d, (axis, sign) in enumerate(dirs):
-        pltpu.make_async_remote_copy(
+    def ask(d, axis, sign):
+        return pltpu.make_async_remote_copy(
             src_ref=req,
             dst_ref=reqs.at[d],
-            send_sem=qs_sem,
-            recv_sem=qr_sem,
+            send_sem=qs_sem.at[d],
+            recv_sem=qr_sem.at[d],
             device_id=neighbour(axis, sign),
             device_id_type=MESH,
-        ).start()
+        )
+
+    for d, (axis, sign) in enumerate(dirs):
+
+        @pl.when(exists(axis, sign))
+        def _():
+            ask(d, axis, sign).start()
+
+    for d, (axis, sign) in enumerate(dirs):
+
+        @pl.when(jnp.logical_not(exists(axis, -sign)))
+        def _():
+            reqs[d] = jnp.zeros(req.shape, f32)
+
+        @pl.when(jnp.logical_not(exists(axis, sign)))
+        def _():
+            for t in range(SWEEPS):
+                drecv[t, d] = jnp.zeros((outer, pairs), f32)
 
     live = jnp.broadcast_to(live_ref[0], (blocks, pairs))
     live_rows = lax.broadcasted_iota(jnp.int32, (blocks, pairs), 0) < live
@@ -190,7 +210,12 @@
         return jnp.concatenate(parts, axis=0)
 
     pos_copy.wait()
-    pltpu.make_async_copy(reqs, reqs, qr_sem).wait()
+    for d, (axis, sign) in enumerate(dirs):
+
+        @pl.when(exists(axis, -sign))
+        def _():
+            ask(d, axis, sign).wait_recv()
+
     asked = []
     for d, (axis, sign) in enumerate(dirs):
         shift = [0, 0, 0]
@@ -207,17 +232,28 @@
         for d, (axis, sign) in enumerate(dirs):
             dsend[t, d] = total[d * outer : (d + 1) * outer]
         for d, (axis, sign) in enumerate(dirs):
-            pltpu.make_async_remote_copy(
-                src_ref=dsend.at[t, d],
-                dst_ref=drecv.at[t, d],
-                send_sem=ds_sem.at[t],
-                recv_sem=dr_sem.at[t],
-                device_id=neighbour(axis, -sign),
-                device_id_type=MESH,
-            ).start()
+
+            @pl.when(exists(axis, -sign))
+            def _():
+                answer(t, d, axis, sign).start()
+
+    def answer(t, d, axis, sign):
+        return pltpu.make_async_remote_copy(
+            src_ref=dsend.at[t, d],
+            dst_ref=drecv.at[t, d],
+            send_sem=ds_sem.at[t, d],
+            recv_sem=dr_sem.at[t, d],
+            device_id=neighbour(axis, -sign),
+            device_id_type=MESH,
+        )
 
     def received(t):
-        pltpu.make_async_copy(drecv.at[t], drecv.at[t], dr_sem.at[t]).wait()
+        for d, (axis, sign) in enumerate(dirs):
+
+            @pl.when(exists(axis, sign))
+            def _():
+                answer(t, d, axis, sign).wait_recv()
+
         got = drecv[t, 0]
         for d in range(1, len(dirs)):
             got = got + drecv[t, d]
@@ -275,8 +311,10 @@
 
     def sweep(t, last):
         depth = jnp.where(live_rows, jnp.maximum(-gap[...], 0.0), 0.0)
-        erecv[t, mine] = lanes_sum(depth * depth)
-        to_all(erecv.at[t, mine], es_sem.at[t], er_sem.at[t])
+        squares = lanes_sum(depth * depth)
+        if not last:
+            erecv[t, mine] = squares
+            to_all(erecv.at[t, mine], es_sem.at[t], er_sem.at[t])
         for g in range(blocks // 8):
             lo, hi = 8 * g, 8 * g + 8
             terms = cat([depth[lo:hi] * geo[c, base + lo : base + hi] for c in range(3)])
@@ -293,13 +331,18 @@
         resid = jnp.sum(lanes_sum(near * near * first_col), axis=1, keepdims=True)
         rrecv[mine] = jnp.where(lane == t, resid, rrecv[mine])
         if last:
+            energy = jnp.sum(squares, axis=1, keepdims=True)
+            rrecv[mine] = jnp.where(lane == SWEEPS, energy, rrecv[mine])
             to_all(rrecv.at[mine], rs_sem, rr_sem)
+            others = rrecv.at[pl.ds(0, devices - 1)]
+            pltpu.make_async_copy(others, others, rr_sem).wait()
+            energy = jnp.sum(rrecv[...], axis=0)[:, SWEEPS : SWEEPS + 1]
         else:
             step = dots(base, 2 * blocks, moved)
             step = step[:blocks] + step[blocks:]
-        others = erecv.at[t, pl.ds(0, devices - 1)]
-        pltpu.make_async_copy(others, others, er_sem.at[t]).wait()
-        energy = jnp.sum(jnp.sum(erecv[t], axis=0), axis=1, keepdims=True)
+            others = erecv.at[t, pl.ds(0, devices - 1)]
+            pltpu.make_async_copy(others, others, er_sem.at[t]).wait()
+            energy = jnp.sum(jnp.sum(erecv[t], axis=0), axis=1, keepdims=True)
         scale = 1.0 / (1.0 + energy / (blocks * pairs * devices))
         hist_ref[0:1, :] = jnp.where(lane == t, energy, hist_ref[0:1, :])
         hist_ref[1:2, :] = jnp.where(lane == t, scale, hist_ref[1:2, :])
@@ -321,14 +364,22 @@
     lax.fori_loop(0, SWEEPS - 1, body, 0)
     sweep(SWEEPS - 1, True)
 
-    pltpu.make_async_copy(reqs, reqs, qs_sem).wait()
-    for t in range(SWEEPS):
-        pltpu.make_async_copy(dsend.at[t], dsend.at[t], ds_sem.at[t]).wait()
+    for d, (axis, sign) in enumerate(dirs):
+
+        @pl.when(exists(axis, sign))
+        def _():
+            ask(d, axis, sign).wait_send()
+
+        @pl.when(exists(axis, -sign))
+        def _():
+            for t in range(SWEEPS):
+                answer(t, d, axis, sign).wait_send()
+
+    for t in range(SWEEPS - 1):
         ref = erecv.at[t, pl.ds(0, devices - 1)]
         pltpu.make_async_copy(ref, ref, es_sem.at[t]).wait()
     others = rrecv.at[pl.ds(0, devices - 1)]
     pltpu.make_async_copy(others, others, rs_sem).wait()
-    pltpu.make_async_copy(others, others, rr_sem).wait()
     energy, scale = hist_ref[0:1, :], hist_ref[1:2, :]
     resid = jnp.sum(rrecv[...], axis=0)
     hist_ref[0:1, :] = jnp.sqrt(1.0 + energy / (blocks * pairs))
@@ -361,9 +412,7 @@
             jax.ShapeDtypeStruct((blocks, 3 * blk[2]), f32),
             jax.ShapeDtypeStruct((8, 128), f32),
         ),
-        in_specs=[vmem] * 6
-
-        + [pl.BlockSpec(memory_space=pl.ANY)],
+        in_specs=[vmem] * 6 + [pl.BlockSpec(memory_space=pl.ANY)],
         out_specs=(vmem, vmem),
         scratch_shapes=[
             pltpu.VMEM(positions.shape, f32),
@@ -384,10 +433,10 @@
             pltpu.VMEM((SWEEPS, devices, 1, 128), f32),
             pltpu.VMEM((devices, 1, 128), f32),
             dma,
-            dma,
-            dma,
-            dma((SWEEPS,)),
-            dma((SWEEPS,)),
+            dma((6,)),
+            dma((6,)),
+            dma((SWEEPS, 6)),
+            dma((SWEEPS, 6)),
             dma((SWEEPS,)),
             dma((SWEEPS,)),
             dma,

time: 56.1 us -> 53.8 us (0.959)
  Pallas kernels: 54.6 us -> 52.3 us
    pallas_call x1, Pallas kernels: 51.4 us -> 49.1 us  [local(): pl.pallas_call(functools.partial(kernel, sizes, blk), out_shape=(jax.Shap...]
where the time goes in v3:
time: 53.8 us; the launch traced here: 53.6 us
  Pallas kernels  52.3 us (97%)
  between operations  1.29 us (2%)
    pallas_call x1, Pallas kernels, local(): pl.pallas_call(functools.partial(kernel, sizes, blk), out_shape=(jax.Shap...  49.1 us
    pallas_call x1, Pallas kernels, local(): pl.pallas_call(finish, grid=(3,), out_shape=(jax.ShapeDtypeStruct(positio...  3.24 us

profile of v3, /device:TPU:0, one launch (start us, length us, event | category | flops | bytes accessed | tf_op | source)
XLA Modules:
  0.0 53.6 jit_solution(14041540000532095033)
XLA Ops:
  1.3 49.1 %shard_map.86 = (f32[32,768]{1,0:T(8,128)}, f32[8,128]{1,0:T(8,128)}) custom-call(s32[1,1,1]{2,1,0:T(1,128)S(6)} %copy.9.live_ref, s32[1,1,1,32,256]{4,3,2,1,0:T(8,128)} %node_ref.1, s32[1,1,1,32]{3,2,1,0:T(1,128)} %line_ref.3, s32[1,1,1,32,256]{4,3,2,1,0:T(8,128)} %farpos_ref.1, s32[1,1,1,32]{3,2,1,0:T(1,128)} %farline_ref.1, ...), custom_call_target="tpu_custom_call" | custom-call | tf_op jit(solution)/shard_map/pallas_call | solution.py:409
  50.3 3.2 %shard_map.87 = (f32[3,16,16,256]{3,2,1,0:T(8,128)}, f32[2,5]{1,0:T(2,128)}) custom-call(f32[32,768]{1,0:T(8,128)} %get-tuple-element.4.acc_ref, s32[1,1,1,32]{3,2,1,0:T(1,128)} %line_ref.3, f32[8,128]{1,0:T(8,128)} %get-tuple-element.5.hist_in, f32[3,16,16,256]{3,2,1,0:T(8,128)} %pos_ref.1), custom_call_target="tpu_custom_call" | custom-call | tf_op jit(solution)/shard_map/pallas_call | solution.py:447

commit v4 on v3

--- a/solution.py
+++ b/solution.py
@@ -112,11 +112,14 @@
         row = ref[0, 0].astype(f32)
         return jnp.transpose(jnp.broadcast_to(row, (pairs, blocks)))
 
-    for c in range(3):
-        req[c] = geom_ref[0, 0, 0, outer:, c, :]
-    req[3] = farpos_ref[0, 0, 0, outer:, :].astype(f32)
+    wide = pairs // 128
+    planes = [geom_ref[0, 0, 0, outer:, c, :] for c in range(3)]
+    planes.append(farpos_ref[0, 0, 0, outer:, :].astype(f32))
+    for c in range(4):
+        for h in range(wide):
+            req[c * wide + h] = planes[c][:, 128 * h : 128 * (h + 1)]
     cols[1] = column(farline_ref)
-    req[4] = cols[1, outer:, :]
+    req[4 * wide] = cols[1, outer:, :128]
     cols[0] = column(line_ref)
     def ask(d, axis, sign):
         return pltpu.make_async_remote_copy(
@@ -220,9 +223,13 @@
     for d, (axis, sign) in enumerate(dirs):
         shift = [0, 0, 0]
         shift[axis] = sign
-        line, z, ok = located(reqs[d, 4], reqs[d, 3], shift)
+        got = [
+            jnp.concatenate([reqs[d, c * wide + h] for h in range(wide)], axis=1) for c in range(4)
+        ]
+        code = jnp.concatenate([reqs[d, 4 * wide]] * wide, axis=1)
+        line, z, ok = located(code, got[3], shift)
         asked.append(
-            [line, jnp.where(ok, z, 0.0)] + [jnp.where(ok, -reqs[d, c], 0.0) for c in range(3)]
+            [line, jnp.where(ok, z, 0.0)] + [jnp.where(ok, -got[c], 0.0) for c in range(3)]
         )
     asked = [cat([x[i] for x in asked]) for i in range(5)]
     base = asked[0].shape[0]
@@ -286,7 +293,7 @@
             ).start()
             return carry
 
-        lax.fori_loop(1, devices, send, 0)
+        lax.fori_loop(1, devices, send, 0, unroll=devices <= 32)
 
     def lanes_sum(x):
         x = jnp.sum(x, axis=0, keepdims=True)
@@ -416,7 +423,7 @@
         out_specs=(vmem, vmem),
         scratch_shapes=[
             pltpu.VMEM(positions.shape, f32),
-            pltpu.VMEM((5, outer, pairs), f32),
+            pltpu.VMEM((4 * (pairs // 128) + 1, outer, 128), f32),
             pltpu.VMEM((2, blocks, pairs), f32),
             pltpu.VMEM((blocks * pairs, blk[2]), bf16),
             pltpu.VMEM((1, 2 * blocks), f32),
@@ -427,7 +434,7 @@
             pltpu.VMEM((rows, pairs), jnp.int32),
             pltpu.VMEM((blocks, pairs), f32),
             pltpu.VMEM((blocks, 3 * blk[2]), f32),
-            pltpu.VMEM((6, 5, outer, pairs), f32),
+            pltpu.VMEM((6, 4 * (pairs // 128) + 1, outer, 128), f32),
             pltpu.VMEM((SWEEPS, 6, outer, pairs), f32),
             pltpu.VMEM((SWEEPS, 6, outer, pairs), f32),
             pltpu.VMEM((SWEEPS, devices, 1, 128), f32),

time: 53.8 us -> 52.2 us (0.970)
  Pallas kernels: 52.3 us -> 50.7 us
    pallas_call x1, Pallas kernels: 49.1 us -> 47.5 us  [local(): pl.pallas_call(functools.partial(kernel, sizes, blk), out_shape=(jax.Shap...]
where the time goes in v4:
time: 52.2 us; the launch traced here: 52 us
  Pallas kernels  50.7 us (97%)
  between operations  1.29 us (2%)
    pallas_call x1, Pallas kernels, local(): pl.pallas_call(functools.partial(kernel, sizes, blk), out_shape=(jax.Shap...  47.5 us
    pallas_call x1, Pallas kernels, local(): pl.pallas_call(finish, grid=(3,), out_shape=(jax.ShapeDtypeStruct(positio...  3.24 us

profile of v4, /device:TPU:0, one launch (start us, length us, event | category | flops | bytes accessed | tf_op | source)
XLA Modules:
  0.0 52.0 jit_solution(6239819224979550876)
XLA Ops:
  1.3 47.5 %shard_map.86 = (f32[32,768]{1,0:T(8,128)}, f32[8,128]{1,0:T(8,128)}) custom-call(s32[1,1,1]{2,1,0:T(1,128)S(6)} %copy.9.live_ref, s32[1,1,1,32,256]{4,3,2,1,0:T(8,128)} %node_ref.1, s32[1,1,1,32]{3,2,1,0:T(1,128)} %line_ref.3, s32[1,1,1,32,256]{4,3,2,1,0:T(8,128)} %farpos_ref.1, s32[1,1,1,32]{3,2,1,0:T(1,128)} %farline_ref.1, ...), custom_call_target="tpu_custom_call" | custom-call | tf_op jit(solution)/shard_map/pallas_call | solution.py:416
  48.8 3.2 %shard_map.87 = (f32[3,16,16,256]{3,2,1,0:T(8,128)}, f32[2,5]{1,0:T(2,128)}) custom-call(f32[32,768]{1,0:T(8,128)} %get-tuple-element.4.acc_ref, s32[1,1,1,32]{3,2,1,0:T(1,128)} %line_ref.3, f32[8,128]{1,0:T(8,128)} %get-tuple-element.5.hist_in, f32[3,16,16,256]{3,2,1,0:T(8,128)} %pos_ref.1), custom_call_target="tpu_custom_call" | custom-call | tf_op jit(solution)/shard_map/pallas_call | solution.py:454
